TPU v7x, 256 devices: a whole 4x4x8 slice. The times are simulated.
256 devices in a mesh: patch: 128 (over y, z, x), sub: 2 (over core).
Axes of the slice: x: 4, y: 4, z: 8, core: 2. Of those that a mesh axis runs over, the one named last changes fastest.
Arguments:
- fields: float32 [5, 512, 128, 128], P(None, ('patch', 'sub')), may hold values from -6 to 6
- density: float32 [512, 128, 128], P(('patch', 'sub')), may hold values from 1 to 3
- moduli: float32 [2, 512, 128, 128], P(None, ('patch', 'sub')), may hold values from 0.5 to 128
- metric_diag: float32 [2, 512, 128, 128], P(None, ('patch', 'sub')), may hold values from 0.7 to 1.3
- metric_cross: float32 [2, 512, 128, 128], P(None, ('patch', 'sub')), may hold values from -0.3 to 0.3
- fc_extension: float32 [25, 10], replicated, may hold values from -2 to 2
- patch_count: int32 [256], P(('patch', 'sub')), may hold values from 1 to 2, as said below
- connectivity: int32 [2048, 3], P(('patch', 'sub')), may hold values from -1 to 255, as said below
Outputs:
- advanced: float32 [5, 512, 128, 128], P(None, ('patch', 'sub'))
Inputs may be any that keep to these rules, and one draw needn't show every extreme that they name: `patch_count`: every device holds at most 2 live patches; the largest count is 2 in every draw. `connectivity`: links join only live slots and are symmetric with equal orientation flags on both ends; a neighbour is held by the same device or by the device whose flat index differs by 1 or 129 modulo 256; from one device to another device go at most 2 linked sides, and this number is reached in every draw.
All inputs are finite; a program needn't handle non-finite values.
Results may differ from a plain program's by a relative error of at most 0.00005.
Values sent between devices are 32-bit elements; how exact they have to be, the bound alone decides.
No kernel may reach another device: no remote copies, remote signals or barrier semaphores. Data moves between devices by JAX's collectives and lax.ppermute only.
A program may use at most 64 MiB of HBM per device.

v0:
```python
import functools

import jax
import jax.numpy as jnp
from jax import lax
from jax.sharding import Mesh
from jax.sharding import PartitionSpec as P

PATCH_SUB = ("patch_0", "patch_1", "patch_2", "sub")
PATCH = ("patch_0", "patch_1", "patch_2")


cfl_number = 0.5
penalty_weight = 0.5


def over_axes(x, axes):
    return functools.reduce(lax.pmax, axes, x)


def shifted(block, axis, distance):
    devices = range(lax.axis_size(axis))
    route = [((i - distance) % len(devices), i) for i in devices]
    return lax.ppermute(block, axis, route)


def wave_speed(density, moduli, metric_diag, metric_cross):
    stiff = moduli[0] + 2.0 * moduli[1]
    xi_norm = jnp.sqrt(metric_diag[0] * metric_diag[0] + metric_cross[0] * metric_cross[0])
    eta_norm = jnp.sqrt(metric_cross[1] * metric_cross[1] + metric_diag[1] * metric_diag[1])
    return jnp.sqrt(stiff / density) * (xi_norm + eta_norm)


def boundary_lines(state):
    stacked = jnp.stack(
        [state[:, :, 0, :], state[:, :, -1, :], state[:, :, :, 0], state[:, :, :, -1]], axis=0
    )
    return jnp.transpose(stacked, (2, 0, 1, 3))


def assemble(
    state, along_xi, along_eta, partner_lines, side_mask, density, moduli, metric_diag, metric_cross
):
    grad_x = metric_diag[0] * along_xi + metric_cross[1] * along_eta
    grad_y = metric_cross[0] * along_xi + metric_diag[1] * along_eta
    lame_first = moduli[0]
    shear = moduli[1]
    stiff = lame_first + 2.0 * shear
    rate_one = (grad_x[2] + grad_y[4]) / density
    rate_two = (grad_x[4] + grad_y[3]) / density
    rate_xx = stiff * grad_x[0] + lame_first * grad_y[1]
    rate_yy = lame_first * grad_x[0] + stiff * grad_y[1]
    rate_xy = shear * (grad_y[0] + grad_x[1])
    rate = jnp.stack([rate_one, rate_two, rate_xx, rate_yy, rate_xy], axis=0)
    points = state.shape[-1]
    jump = (
        penalty_weight
        * (points - 1)
        * (partner_lines - boundary_lines(state))
        * side_mask[:, :, None, None]
    )
    jump = jnp.transpose(jump, (1, 2, 0, 3))
    rate = rate.at[:, :, 0, :].add(jump[0])
    rate = rate.at[:, :, points - 1, :].add(jump[1])
    rate = rate.at[:, :, :, 0].add(jump[2])
    rate = rate.at[:, :, :, points - 1].add(jump[3])
    return rate


def derivative_matrix(extension, points):
    extra_cols = extension.shape[0]
    match_pts = extension.shape[1] // 2
    length = points + extra_cols
    half_len = (length - 1) // 2
    row_ids = jnp.arange(length, dtype=jnp.int32)[:, None]
    col_ids = jnp.arange(length, dtype=jnp.int32)[None, :]
    wave_ids = jnp.arange(1, half_len + 1, dtype=jnp.int32)
    phase_int = wave_ids[:, None, None] * (row_ids - col_ids)[None] % length
    angles = 2.0 * jnp.pi / length * phase_int.astype(jnp.float32)
    weights = wave_ids.astype(jnp.float32) * (2.0 * jnp.pi * (points - 1) / length)
    kernel = -(2.0 / length) * jnp.sum(weights[:, None, None] * jnp.sin(angles), axis=0)
    inner_part = kernel[:points, :points]
    outer_part = kernel[:points, points:]
    folded = jnp.dot(
        outer_part, extension, precision=lax.Precision.HIGHEST, preferred_element_type=jnp.float32
    )
    inner_part = inner_part.at[:, points - match_pts :].add(folded[:, :match_pts])
    inner_part = inner_part.at[:, :match_pts].add(folded[:, match_pts:])
    return inner_part


def shards(
    fields, density, moduli, metric_diag, metric_cross, fc_extension, patch_count, connectivity
):
    points = fields.shape[-1]
    components = fields.shape[0]
    slot_count = fields.shape[1]
    operator = derivative_matrix(fc_extension, points)
    live = jnp.arange(slot_count, dtype=jnp.int32) < patch_count[0]
    speeds = wave_speed(density, moduli, metric_diag, metric_cross)
    local_bound = jnp.max(jnp.where(live[:, None, None], speeds, jnp.float32(0.0)))
    bound = over_axes(local_bound, PATCH_SUB)
    time_step = cfl_number / (bound * (points - 1))
    owner = connectivity[:, 0]
    strip_index = connectivity[:, 1]
    flipped = connectivity[:, 2] == 1
    side_mask = (owner >= 0).astype(jnp.float32).reshape(slot_count, 4)
    myself = lax.axis_index(PATCH_SUB)
    patch_total = lax.axis_size(PATCH)
    sub_total = lax.axis_size("sub")
    device_total = patch_total * sub_total
    far_step = device_total // 2 + 1
    positions = jnp.arange(owner.shape[0], dtype=jnp.int32)
    same_owner = owner[:, None] == owner[None, :]
    send_rank = jnp.sum(same_owner & (positions[None, :] < positions[:, None]), axis=1)
    recv_pos = jnp.sum(same_owner & (strip_index[None, :] < strip_index[:, None]), axis=1)
    line_shape = (components, points)

    def partner_lines(state):
        own_lines = boundary_lines(state).reshape((slot_count * 4,) + line_shape)
        result = own_lines[strip_index]
        for offset in (1, -1, far_step, -far_step):
            chosen = owner == (myself + offset) % device_total
            target = jnp.where(chosen, send_rank, slot_count)
            outbox = (
                jnp.zeros((slot_count,) + line_shape, jnp.float32)
                .at[target]
                .set(own_lines, mode="drop")
            )
            arrived = shifted(outbox, PATCH_SUB, offset)
            source = owner == (myself - offset) % device_total
            result = jnp.where(
                source[:, None, None], arrived[jnp.minimum(recv_pos, slot_count - 1)], result
            )
        result = jnp.where(flipped[:, None, None], result[..., ::-1], result)
        return result.reshape((slot_count, 4) + line_shape)

    def rates(state):
        neighbours = partner_lines(state)
        along_xi = jnp.einsum("ij,cpjk->cpik", operator, state, precision=lax.Precision.HIGHEST)
        along_eta = jnp.einsum("kl,cpjl->cpjk", operator, state, precision=lax.Precision.HIGHEST)
        return assemble(
            state,
            along_xi,
            along_eta,
            neighbours,
            side_mask,
            density,
            moduli,
            metric_diag,
            metric_cross,
        )

    middle = fields + time_step * rates(fields)
    final = middle + time_step * rates(middle)
    return jnp.where(live[None, :, None, None], 0.5 * (fields + final), jnp.float32(0.0))


def solution(mesh):
    torus = Mesh(
        mesh.devices.reshape(4, 8, 4, mesh.shape["sub"]), ("patch_0", "patch_1", "patch_2", "sub")
    )
    return jax.shard_map(
        shards,
        mesh=torus,
        in_specs=(
            P(None, PATCH_SUB, None, None),
            P(PATCH_SUB, None, None),
            P(None, PATCH_SUB, None, None),
            P(None, PATCH_SUB, None, None),
            P(None, PATCH_SUB, None, None),
            P(),
            P(PATCH_SUB),
            P(PATCH_SUB, None),
        ),
        out_specs=P(None, PATCH_SUB, None, None),
        check_vma=False,
    )
```

profile of v0, /device:TPU:8, one launch (start us, length us, event | category | flops | bytes accessed | tf_op | source)
XLA Modules:
  0.0 164.4 jit_solution(2622845855082754663)
XLA Ops:
  0.0 1.6 fusion.56
  2.5 0.7 scatter_fusion
  3.2 8.6 %collective-permute-start = (f32[2,5,128]{2,1,0:T(8,128)S(1)}, f32[2,5,128]{2,1,0:T(8,128)S(1)}, u32[]{:S(2)}, u32[]{:S(2)}) collective-permute-start(f32[2,5,128]{2,1,0:T(8,128)S(1)} %scatter_fusion), channel_id=1, source_target_pairs={{129,0},{130,1},{131,2},{132,3},{133,4},{134,5},{135,6},{136,7},{1... | collective-permute-start | bytes 15368 | tf_op jit(solution)/shard_map/ppermute | solution.py:24
  12.7 0.7 scatter_fusion.2
  13.4 6.1 %collective-permute-start.2 = (f32[2,5,128]{2,1,0:T(8,128)S(1)}, f32[2,5,128]{2,1,0:T(8,128)S(1)}, u32[]{:S(2)}, u32[]{:S(2)}) collective-permute-start(f32[2,5,128]{2,1,0:T(8,128)S(1)} %scatter_fusion.2), channel_id=1, source_target_pairs={{1,0},{2,1},{3,2},{4,3},{5,4},{6,5},{7,6},{8,7},{9,8},{10,9},{11,1... | collective-permute-start | bytes 15368 | tf_op jit(solution)/shard_map/ppermute | solution.py:24
  21.6 49.5 %fusion.4 = f32[153,153]{1,0:T(8,128)S(1)} fusion(s32[153,153]{1,0:T(8,128)S(1)} %iota_subtract_fusion, s32[76]{0:T(128)S(1)} %iota_add_fusion, f32[76]{0:T(128)S(1)} %convert_multiply_fusion), kind=kLoop, calls=%fused_computation.23 | loop fusion | flops 19546516 | bytes 187880 | tf_op jit(solution)/shard_map/reduce_sum | solution.py:81
  73.5 0.8 multiply_add_fusion.4
  75.3 0.8 fusion.31
  76.3 10.1 %pmax.28 = f32[]{:T(128)} all-reduce(f32[]{:T(128)} %get-tuple-element.129), channel_id=1, replica_groups=mesh['patch_0'=4,'patch_1'=8,'patch_2'=4,'sub'=2] {'patch_0'}, use_global_device_ids=true, to_apply=%region_1.2 | all-reduce | flops 1 | bytes 8 | tf_op jit(solution)/shard_map/pmax | solution.py:18
  86.3 14.7 %pmax.29 = f32[]{:T(128)} all-reduce(f32[]{:T(128)} %pmax.28), channel_id=1, replica_groups=mesh['patch_0'=4,'patch_1'=8,'patch_2'=4,'sub'=2] {'patch_1'}, use_global_device_ids=true, to_apply=%region_2.3 | all-reduce | flops 1 | bytes 8 | tf_op jit(solution)/shard_map/pmax | solution.py:18
  101.0 8.3 %pmax.30 = f32[]{:T(128)} all-reduce(f32[]{:T(128)} %pmax.29), channel_id=1, replica_groups=mesh['patch_0'=4,'patch_1'=8,'patch_2'=4,'sub'=2] {'patch_2'}, use_global_device_ids=true, to_apply=%region_3.4 | all-reduce | flops 1 | bytes 8 | tf_op jit(solution)/shard_map/pmax | solution.py:18
  109.3 3.0 %pmax.31 = f32[]{:T(128)} all-reduce(f32[]{:T(128)} %pmax.30), channel_id=1, replica_groups=mesh['patch_0'=4,'patch_1'=8,'patch_2'=4,'sub'=2] {'sub'}, use_global_device_ids=true, to_apply=%region_4.5 | all-reduce | flops 1 | bytes 8 | tf_op jit(solution)/shard_map/pmax | solution.py:18
  117.2 4.2 %scatter-add.40 = f32[5,2,128,128]{3,2,1,0:T(8,128)S(1)} dynamic-update-slice(f32[5,2,128,128]{3,2,1,0:T(8,128)S(1)} %scatter-add.39, f32[5,2,128,1]{3,2,1,0:T(8,128)S(1)} %copy.243, s32[]{:T(128)} %constant.341.clone.1, s32[]{:T(128)} %constant.341.clone.1, s32[]{:T(128)} %constant.341.clone.1, s32[]{:T(128)} %constant.341.clone.1) | dynamic-update-slice | bytes 10244 | tf_op jit(solution)/shard_map/scatter-add | solution.py:65
  122.2 5.1 %scatter-add.41 = f32[5,2,128,128]{3,2,1,0:T(8,128)S(1)} dynamic-update-slice(f32[5,2,128,128]{3,2,1,0:T(8,128)S(1)} %scatter-add.40, f32[5,2,128,1]{3,2,1,0:T(8,128)S(1)} %copy.245, s32[]{:T(128)} %constant.341.clone.1, s32[]{:T(128)} %constant.341.clone.1, s32[]{:T(128)} %constant.341.clone.1, s32[]{:T(128)} %constant.359.clone.1) | dynamic-update-slice | bytes 10244 | tf_op jit(solution)/shard_map/scatter-add | solution.py:66
  129.1 0.8 multiply_add_fusion.1
  130.8 0.7 scatter_fusion.4
  131.6 2.3 %collective-permute-start.4 = (f32[2,5,128]{2,1,0:T(8,128)S(1)}, f32[2,5,128]{2,1,0:T(8,128)S(1)}, u32[]{:S(2)}, u32[]{:S(2)}) collective-permute-start(f32[2,5,128]{2,1,0:T(8,128)S(1)} %scatter_fusion.4), channel_id=1, source_target_pairs={{129,0},{130,1},{131,2},{132,3},{133,4},{134,5},{135,6},{136,7},{1... | collective-permute-start | bytes 15368 | tf_op jit(solution)/shard_map/ppermute | solution.py:24
  134.6 1.1 collective-permute-start.5
  136.5 7.4 %collective-permute-start.6 = (f32[2,5,128]{2,1,0:T(8,128)S(1)}, f32[2,5,128]{2,1,0:T(8,128)S(1)}, u32[]{:S(2)}, u32[]{:S(2)}) collective-permute-start(f32[2,5,128]{2,1,0:T(8,128)S(1)} %scatter_fusion.6), channel_id=1, source_target_pairs={{1,0},{2,1},{3,2},{4,3},{5,4},{6,5},{7,6},{8,7},{9,8},{10,9},{11,1... | collective-permute-start | bytes 15368 | tf_op jit(solution)/shard_map/ppermute | solution.py:24
  144.7 0.9 fusion.9
  148.1 3.9 %collective-permute-done.7 = f32[2,5,128]{2,1,0:T(8,128)S(1)} collective-permute-done((f32[2,5,128]{2,1,0:T(8,128)S(1)}, f32[2,5,128]{2,1,0:T(8,128)S(1)}, u32[]{:S(2)}, u32[]{:S(2)}) %collective-permute-start.7) | collective-permute-done | bytes 5152 | tf_op jit(solution)/shard_map/ppermute | solution.py:24
  153.4 4.2 %scatter-add.46 = f32[5,2,128,128]{3,2,1,0:T(8,128)S(1)} dynamic-update-slice(f32[5,2,128,128]{3,2,1,0:T(8,128)S(1)} %scatter-add.45, f32[5,2,128,1]{3,2,1,0:T(8,128)S(1)} %slice_add_fusion.1, s32[]{:T(128)} %constant.341.clone.1, s32[]{:T(128)} %constant.341.clone.1, s32[]{:T(128)} %constant.341.clone.1, s32[]{:T(128)} %constant.341.clone.1) | dynamic-update-slice | bytes 10244 | tf_op jit(solution)/shard_map/scatter-add | solution.py:65
  158.2 5.1 %scatter-add.49 = f32[5,2,128,128]{3,2,1,0:T(8,128)S(1)} dynamic-update-slice(f32[5,2,128,128]{3,2,1,0:T(8,128)S(1)} %scatter-add.46, f32[5,2,128,1]{3,2,1,0:T(8,128)S(1)} %slice_add_fusion, s32[]{:T(128)} %constant.341.clone.1, s32[]{:T(128)} %constant.341.clone.1, s32[]{:T(128)} %constant.341.clone.1, s32[]{:T(128)} %constant.359.clone.1) | dynamic-update-slice | bytes 10244 | tf_op jit(solution)/shard_map/scatter-add | solution.py:66
  163.3 1.1 multiply_select_fusion
  (176 shorter events, 20.3 us)
Async XLA Ops:
  0.0 71.3 %copy-start = (f32[25,10]{0,1:T(8,128)S(1)}, f32[25,10]{0,1:T(8,128)}, u32[]{:S(2)}) copy-start(f32[25,10]{0,1:T(8,128)} %param.33) | copy-start | bytes 3004
  2.4 9.4 %copy-start.24 = (s32[8]{0:T(128)}, s32[8]{0:T(128)S(1)}, u32[]{:S(2)}) copy-start(s32[8]{0:T(128)S(1)} %get-tuple-element.150) | copy-start | bytes 100
  2.5 9.4 %copy-start.26 = (s32[8]{0:T(128)}, s32[8]{0:T(128)S(1)}, u32[]{:S(2)}) copy-start(s32[8]{0:T(128)S(1)} %get-tuple-element.152) | copy-start | bytes 100
  2.5 17.1 %copy-start.20 = (s32[8]{0:T(128)}, s32[8]{0:T(128)S(1)}, u32[]{:S(2)}) copy-start(s32[8]{0:T(128)S(1)} %get-tuple-element.149) | copy-start | bytes 100
  2.5 17.1 %copy-start.22 = (s32[8]{0:T(128)}, s32[8]{0:T(128)S(1)}, u32[]{:S(2)}) copy-start(s32[8]{0:T(128)S(1)} %get-tuple-element.151) | copy-start | bytes 100
  3.2 110.5 %collective-permute-start = (f32[2,5,128]{2,1,0:T(8,128)S(1)}, f32[2,5,128]{2,1,0:T(8,128)S(1)}, u32[]{:S(2)}, u32[]{:S(2)}) collective-permute-start(f32[2,5,128]{2,1,0:T(8,128)S(1)} %scatter_fusion), channel_id=1, source_target_pairs={{129,0},{130,1},{131,2},{132,3},{133,4},{134,5},{135,6},{136,7},{1... | collective-permute-start | bytes 15368 | tf_op jit(solution)/shard_map/ppermute | solution.py:24
  12.6 101.7 %collective-permute-start.1 = (f32[2,5,128]{2,1,0:T(8,128)S(1)}, f32[2,5,128]{2,1,0:T(8,128)S(1)}, u32[]{:S(2)}, u32[]{:S(2)}) collective-permute-start(f32[2,5,128]{2,1,0:T(8,128)S(1)} %scatter_fusion.1), channel_id=1, source_target_pairs={{127,0},{128,1},{129,2},{130,3},{131,4},{132,5},{133,6},{134,7},{1... | collective-permute-start | bytes 15368 | tf_op jit(solution)/shard_map/ppermute | solution.py:24
  13.4 101.5 %collective-permute-start.2 = (f32[2,5,128]{2,1,0:T(8,128)S(1)}, f32[2,5,128]{2,1,0:T(8,128)S(1)}, u32[]{:S(2)}, u32[]{:S(2)}) collective-permute-start(f32[2,5,128]{2,1,0:T(8,128)S(1)} %scatter_fusion.2), channel_id=1, source_target_pairs={{1,0},{2,1},{3,2},{4,3},{5,4},{6,5},{7,6},{8,7},{9,8},{10,9},{11,1... | collective-permute-start | bytes 15368 | tf_op jit(solution)/shard_map/ppermute | solution.py:24
  20.3 95.2 %collective-permute-start.3 = (f32[2,5,128]{2,1,0:T(8,128)S(1)}, f32[2,5,128]{2,1,0:T(8,128)S(1)}, u32[]{:S(2)}, u32[]{:S(2)}) collective-permute-start(f32[2,5,128]{2,1,0:T(8,128)S(1)} %scatter_fusion.3), channel_id=1, source_target_pairs={{255,0},{0,1},{1,2},{2,3},{3,4},{4,5},{5,6},{6,7},{7,8},{8,9},{9,1... | collective-permute-start | bytes 15368 | tf_op jit(solution)/shard_map/ppermute | solution.py:24
  76.1 39.9 %copy-start.12 = (pred[8]{0:T(512)(128)(4,1)S(1)}, pred[8]{0:T(512)(128)(4,1)}, u32[]{:S(2)}) copy-start(pred[8]{0:T(512)(128)(4,1)} %get-tuple-element.153) | copy-start | bytes 28
  76.2 39.9 %copy-start.14 = (pred[8]{0:T(512)(128)(4,1)S(1)}, pred[8]{0:T(512)(128)(4,1)}, u32[]{:S(2)}) copy-start(pred[8]{0:T(512)(128)(4,1)} %get-tuple-element.154) | copy-start | bytes 28
  76.2 39.9 %copy-start.16 = (pred[8]{0:T(512)(128)(4,1)S(1)}, pred[8]{0:T(512)(128)(4,1)}, u32[]{:S(2)}) copy-start(pred[8]{0:T(512)(128)(4,1)} %get-tuple-element.155) | copy-start | bytes 28
  76.2 39.9 %copy-start.18 = (pred[8]{0:T(512)(128)(4,1)S(1)}, pred[8]{0:T(512)(128)(4,1)}, u32[]{:S(2)}) copy-start(pred[8]{0:T(512)(128)(4,1)} %get-tuple-element.156) | copy-start | bytes 28
  86.3 30.6 %copy-start.31 = (pred[8]{0:T(512)(128)(4,1)}, pred[8]{0:T(512)(128)(4,1)S(1)}, u32[]{:S(2)}) copy-start(pred[8]{0:T(512)(128)(4,1)S(1)} %compare_bitcast_fusion) | copy-start | bytes 28
  130.0 13.9 %copy-start.21 = (s32[8]{0:T(128)S(1)}, s32[8]{0:T(128)}, u32[]{:S(2)}) copy-start(s32[8]{0:T(128)} %copy-done.20) | copy-start | bytes 100
  130.8 21.8 %copy-start.13 = (pred[8]{0:T(512)(128)(4,1)S(1)}, pred[8]{0:T(512)(128)(4,1)}, u32[]{:S(2)}) copy-start(pred[8]{0:T(512)(128)(4,1)} %get-tuple-element.153) | copy-start | bytes 28
  130.8 21.8 %copy-start.15 = (pred[8]{0:T(512)(128)(4,1)S(1)}, pred[8]{0:T(512)(128)(4,1)}, u32[]{:S(2)}) copy-start(pred[8]{0:T(512)(128)(4,1)} %get-tuple-element.154) | copy-start | bytes 28
  130.8 21.8 %copy-start.17 = (pred[8]{0:T(512)(128)(4,1)S(1)}, pred[8]{0:T(512)(128)(4,1)}, u32[]{:S(2)}) copy-start(pred[8]{0:T(512)(128)(4,1)} %get-tuple-element.155) | copy-start | bytes 28
  130.8 21.8 %copy-start.19 = (pred[8]{0:T(512)(128)(4,1)S(1)}, pred[8]{0:T(512)(128)(4,1)}, u32[]{:S(2)}) copy-start(pred[8]{0:T(512)(128)(4,1)} %get-tuple-element.156) | copy-start | bytes 28
  131.6 14.8 %collective-permute-start.4 = (f32[2,5,128]{2,1,0:T(8,128)S(1)}, f32[2,5,128]{2,1,0:T(8,128)S(1)}, u32[]{:S(2)}, u32[]{:S(2)}) collective-permute-start(f32[2,5,128]{2,1,0:T(8,128)S(1)} %scatter_fusion.4), channel_id=1, source_target_pairs={{129,0},{130,1},{131,2},{132,3},{133,4},{134,5},{135,6},{136,7},{1... | collective-permute-start | bytes 15368 | tf_op jit(solution)/shard_map/ppermute | solution.py:24
  134.6 12.3 %collective-permute-start.5 = (f32[2,5,128]{2,1,0:T(8,128)S(1)}, f32[2,5,128]{2,1,0:T(8,128)S(1)}, u32[]{:S(2)}, u32[]{:S(2)}) collective-permute-start(f32[2,5,128]{2,1,0:T(8,128)S(1)} %scatter_fusion.5), channel_id=1, source_target_pairs={{127,0},{128,1},{129,2},{130,3},{131,4},{132,5},{133,6},{134,7},{1... | collective-permute-start | bytes 15368 | tf_op jit(solution)/shard_map/ppermute | solution.py:24
  135.7 17.1 %copy-start.32 = (pred[8]{0:T(512)(128)(4,1)S(1)}, pred[8]{0:T(512)(128)(4,1)}, u32[]{:S(2)}) copy-start(pred[8]{0:T(512)(128)(4,1)} %copy-done.31) | copy-start | bytes 28
  136.5 11.0 %collective-permute-start.6 = (f32[2,5,128]{2,1,0:T(8,128)S(1)}, f32[2,5,128]{2,1,0:T(8,128)S(1)}, u32[]{:S(2)}, u32[]{:S(2)}) collective-permute-start(f32[2,5,128]{2,1,0:T(8,128)S(1)} %scatter_fusion.6), channel_id=1, source_target_pairs={{1,0},{2,1},{3,2},{4,3},{5,4},{6,5},{7,6},{8,7},{9,8},{10,9},{11,1... | collective-permute-start | bytes 15368 | tf_op jit(solution)/shard_map/ppermute | solution.py:24
  144.6 7.4 %collective-permute-start.7 = (f32[2,5,128]{2,1,0:T(8,128)S(1)}, f32[2,5,128]{2,1,0:T(8,128)S(1)}, u32[]{:S(2)}, u32[]{:S(2)}) collective-permute-start(f32[2,5,128]{2,1,0:T(8,128)S(1)} %scatter_fusion.7), channel_id=1, source_target_pairs={{255,0},{0,1},{1,2},{2,3},{3,4},{4,5},{5,6},{6,7},{7,8},{8,9},{9,1... | collective-permute-start | bytes 15368 | tf_op jit(solution)/shard_map/ppermute | solution.py:24
  (17 other events, 31.6 us)
where the time goes:
time: 165 us; the launch traced here: 164 us
  other arithmetic  55.8 us (34%)
  local copies, waits for them, and re-layouts  37.3 us (23%)
  blocking collectives  36 us (22%)
  starting transfers between devices  25.8 us (16%)
  waiting for transfers between devices  3.96 us (2%)
  matrix products  3.13 us (2%)
  between operations  2.37 us (1%)
    reduce_sum x1, other arithmetic, derivative_matrix(): jnp.sum(weights[:, None, None] * jnp.sin(angles), axis=0)  49.5 us
    pmax x4, blocking collectives, over_axes(): return functools.reduce(lax.pmax, axes, x)  36 us
    ppermute x8, starting transfers between devices, shifted(): return lax.ppermute(block, axis, route)  25.8 us
    scatter-add x2, local copies, waits for them, and re-layouts, assemble(): rate = rate.at[:, :, :, points - 1].add(jump[3])  10.2 us
    scatter-add x2, local copies, waits for them, and re-layouts, assemble(): rate = rate.at[:, :, :, 0].add(jump[2])  8.37 us
    scatter x8, local copies, waits for them, and re-layouts, partner_lines(): outbox = jnp.zeros((slot_count,) + line_shape, jnp.float32).at[target].se...  5.91 us
    gather x8, local copies, waits for them, and re-layouts, partner_lines(): arrived[jnp.minimum(recv_pos, slot_count - 1)]  4.44 us
    ppermute x8, waiting for transfers between devices, shifted(): return lax.ppermute(block, axis, route)  3.96 us
  transfers between devices with their start and end apart: 8, of which 1 were waited for; matrix products, arithmetic and copies ran while one was open for 39% of the time, Pallas kernels for 0%

commit v1 on v0

v1 whole, which is shorter than its diff:
```python
import functools

import jax
import jax.numpy as jnp
import numpy as np
from jax import lax
from jax.experimental import pallas as pl
from jax.experimental.pallas import tpu as pltpu
from jax.sharding import Mesh
from jax.sharding import PartitionSpec as P

PATCH_SUB = ("patch_0", "patch_1", "patch_2", "sub")

CFL = 0.5
PENALTY = 0.5
CHUNK = 16
F32 = jnp.float32
BF16 = jnp.bfloat16
VMEM = pl.BlockSpec(memory_space=pltpu.VMEM)
SMEM = pl.BlockSpec(memory_space=pltpu.SMEM)
PARAMS = pltpu.CompilerParams(vmem_limit_bytes=12 * 1024 * 1024)


def fourier_matrix(points, cont):
    length = points + cont
    delta = np.arange(points)[:, None] - np.arange(length)[None, :]
    safe = np.where(delta == 0, 1, delta)
    scale = np.pi * (points - 1) / length
    sign = np.where(delta % 2 == 0, 1.0, -1.0)
    full = np.where(delta == 0, 0.0, scale * sign / np.sin(np.pi * safe / length))
    return full[:, :points].astype(np.float32), full[:, points:].astype(np.float32)


def pair_offsets(step):
    return (1, -1, step, -step)


def swap_routes(total, step):
    routes = []
    for offset in pair_offsets(step):
        route = []
        for i in range(total):
            target = (i + offset) % total if i % 2 == 0 else (i - offset) % total
            route.append((i, target))
        routes.append(route)
    return routes


def partner_ids(me, total, step):
    sign = jnp.where(me % 2 == 0, 1, -1)
    return [lax.rem(me + sign * offset + 2 * total, total) for offset in pair_offsets(step)]


def lane_ids(shape):
    return lax.broadcasted_iota(jnp.int32, shape, len(shape) - 1)


def extract_lines(load, own_ref, scr_ref, fields, slots, points):
    lanes = lane_ids((points, points))
    columns = jnp.zeros((points, points), F32)
    for s in range(slots):
        for f in range(fields):
            at = 2 * (s * fields + f)
            moved = pltpu.roll(load(f, s), at + 1, 1)
            columns = jnp.where((lanes == at) | (lanes == at + 1), moved, columns)
    scr_ref[...] = columns.T
    for s in range(slots):
        base = 2 * s * fields
        own_ref[4 * s + 2, pl.ds(0, fields), :] = scr_ref[pl.ds(base + 1, fields, stride=2), :]
        own_ref[4 * s + 3, pl.ds(0, fields), :] = scr_ref[pl.ds(base, fields, stride=2), :]


def fill_outboxes(own_ref, out_refs, conn_ref, partners):
    sides = own_ref.shape[0]
    for partner, out_ref in zip(partners, out_refs):
        first = jnp.int32(0)
        second = jnp.int32(0)
        count = jnp.int32(0)
        for i in range(sides):
            match = conn_ref[i, 0] == partner
            first = jnp.where(match & (count == 0), i, first)
            second = jnp.where(match & (count == 1), i, second)
            count = count + match.astype(jnp.int32)
        out_ref[0] = own_ref[first]
        out_ref[1] = own_ref[second]


def jumps(own_ref, in_refs, table_ref, jump_ref, conn_ref, me, partners, points, scale):
    sides = own_ref.shape[0]
    for i in range(sides):
        table_ref[i] = own_ref[i]
    for k, in_ref in enumerate(in_refs):
        table_ref[sides + 2 * k] = in_ref[0]
        table_ref[sides + 2 * k + 1] = in_ref[1]
    lanes = lane_ids((8, points))
    for i in range(sides):
        owner = conn_ref[i, 0]
        strip = conn_ref[i, 1]
        position = jnp.int32(0)
        for j in range(sides):
            if j != i:
                before = (conn_ref[j, 0] == owner) & (conn_ref[j, 1] < strip)
                position = position + before.astype(jnp.int32)
        place = strip
        for k, partner in enumerate(partners):
            place = jnp.where(owner == partner, sides + 2 * k + position, place)
        place = jnp.clip(place, 0, 2 * sides - 1)
        line = table_ref[place]
        index = jnp.where(conn_ref[i, 2] == 1, points - 1 - lanes, lanes)
        line = jnp.take_along_axis(line, index, axis=1)
        weight = jnp.where(owner >= 0, scale, 0.0).astype(F32)
        jump_ref[i] = weight * (line - own_ref[i])


def jump_columns(jump_ref, scr_ref, fields, slots, points):
    scr_ref[...] = jnp.zeros(scr_ref.shape, F32)
    for s in range(slots):
        base = 2 * s * fields
        for f in range(fields):
            scr_ref[pl.ds(base + 2 * f + 1, 1), :] = jump_ref[4 * s + 2, pl.ds(f, 1), :]
            scr_ref[pl.ds(base + 2 * f, 1), :] = jump_ref[4 * s + 3, pl.ds(f, 1), :]
    return scr_ref[...].T


def lines_kernel(
    fields_ref, density_ref, moduli_ref, diag_ref, cross_ref, conn_ref, count_ref, me_ref,
    out0, out1, out2, out3, own_ref, peak_ref, scr_ref, *, total, step,
):
    fields, slots, points, _ = fields_ref.shape
    for s in range(slots):
        for f in range(fields):
            own_ref[4 * s, pl.ds(f, 1), :] = fields_ref[f, s, pl.ds(0, 1), :]
            own_ref[4 * s + 1, pl.ds(f, 1), :] = fields_ref[f, s, pl.ds(points - 1, 1), :]
    extract_lines(lambda f, s: fields_ref[f, s], own_ref, scr_ref, fields, slots, points)
    fill_outboxes(own_ref, (out0, out1, out2, out3), conn_ref, partner_ids(me_ref[0], total, step))

    peak = jnp.zeros((8, points), F32)
    for s in range(slots):
        live = s < count_ref[0]

        def body(c, peak, s=s, live=live):
            rows = pl.ds(pl.multiple_of(c * CHUNK, CHUNK), CHUNK)
            stiff = moduli_ref[0, s, rows, :] + 2.0 * moduli_ref[1, s, rows, :]
            xi_x, eta_y = diag_ref[0, s, rows, :], diag_ref[1, s, rows, :]
            xi_y, eta_x = cross_ref[0, s, rows, :], cross_ref[1, s, rows, :]
            speed = jnp.sqrt(stiff / density_ref[s, rows, :]) * (
                jnp.sqrt(xi_x * xi_x + xi_y * xi_y) + jnp.sqrt(eta_x * eta_x + eta_y * eta_y)
            )
            speed = jnp.where(live, speed, 0.0)
            for r in range(CHUNK // 8):
                peak = jnp.maximum(peak, speed[8 * r : 8 * r + 8])
            return peak

        peak = lax.fori_loop(0, points // CHUNK, body, peak, unroll=True)
    row = jnp.max(peak, axis=0, keepdims=True)
    peak_ref[...] = jnp.broadcast_to(row, peak_ref.shape)


def matrix_kernel(inner_ref, outer_ref, ext_ref, left_ref, right_ref):
    points = inner_ref.shape[0]
    match = ext_ref.shape[1] // 2
    rows = lax.broadcasted_iota(jnp.int32, (2 * match, points), 0)
    lanes = lane_ids((2 * match, points))
    spread = jnp.where(lanes == jnp.where(rows < match, points - match + rows, rows - match), 1.0, 0.0)
    dot = functools.partial(
        jnp.dot, precision=lax.Precision.HIGHEST, preferred_element_type=F32
    )
    full = inner_ref[...] + dot(outer_ref[...], dot(ext_ref[...], spread.astype(F32)))
    high = full.astype(BF16)
    low = (full - high.astype(F32)).astype(BF16)
    zero = jnp.zeros((points, points), BF16)
    left_ref[pl.ds(0, points), pl.ds(0, points)] = high
    left_ref[pl.ds(0, points), pl.ds(points, points)] = high
    left_ref[pl.ds(points, points), pl.ds(0, points)] = low
    left_ref[pl.ds(points, points), pl.ds(points, points)] = zero
    turned = full.T
    high = turned.astype(BF16)
    low = (turned - high.astype(F32)).astype(BF16)
    right_ref[pl.ds(0, points), pl.ds(0, points)] = high
    right_ref[pl.ds(points, points), pl.ds(0, points)] = high
    right_ref[pl.ds(0, points), pl.ds(points, points)] = low
    right_ref[pl.ds(points, points), pl.ds(points, points)] = zero


def derivatives(load, left_ref, right_ref, cols_ref, rows_ref, xi_ref, eta_ref, fields, slots, points):
    for f in range(fields):
        for s in range(slots):
            value = load(f, s)
            high = value.astype(BF16)
            low = (value - high.astype(F32)).astype(BF16)
            cols_ref[f, pl.ds(0, points), pl.ds(s * points, points)] = high
            cols_ref[f, pl.ds(points, points), pl.ds(s * points, points)] = low
            rows_ref[f, pl.ds(s * points, points), pl.ds(0, points)] = high
            rows_ref[f, pl.ds(s * points, points), pl.ds(points, points)] = low
        got = jnp.dot(left_ref[...], cols_ref[f], preferred_element_type=F32)
        along = got[:points] + got[points:]
        for s in range(slots):
            xi_ref[f, s] = along[:, s * points : (s + 1) * points]
        got = jnp.dot(rows_ref[f], right_ref[...], preferred_element_type=F32)
        along = got[:, :points] + got[:, points:]
        for s in range(slots):
            eta_ref[f, s] = along[s * points : (s + 1) * points]


def assemble(s, rows, density_ref, moduli_ref, diag_ref, cross_ref, xi_ref, eta_ref):
    xi_x, eta_y = diag_ref[0, s, rows, :], diag_ref[1, s, rows, :]
    xi_y, eta_x = cross_ref[0, s, rows, :], cross_ref[1, s, rows, :]
    lame, shear = moduli_ref[0, s, rows, :], moduli_ref[1, s, rows, :]
    light = 1.0 / density_ref[s, rows, :]
    stiff = lame + 2.0 * shear

    def dx(f):
        return xi_x * xi_ref[f, s, rows, :] + eta_x * eta_ref[f, s, rows, :]

    def dy(f):
        return xi_y * xi_ref[f, s, rows, :] + eta_y * eta_ref[f, s, rows, :]

    one_x, two_y = dx(0), dy(1)
    return (
        (dx(2) + dy(4)) * light,
        (dx(4) + dy(3)) * light,
        stiff * one_x + lame * two_y,
        lame * one_x + stiff * two_y,
        shear * (dy(0) + dx(1)),
    )


def column_part(turned, at, points):
    moved = pltpu.roll(turned, points - 1 - at, 1)
    lanes = lane_ids(moved.shape)
    return jnp.where((lanes == 0) | (lanes == points - 1), moved, 0.0)


def first_kernel(
    fields_ref, density_ref, moduli_ref, diag_ref, cross_ref, left_ref, right_ref, own_ref,
    in0, in1, in2, in3, conn_ref, me_ref,
    rate_ref, out0, out1, out2, out3, mine_ref,
    table_ref, jump_ref, scr_ref, turned_ref, cols_ref, rows_ref, xi_ref, eta_ref, *, total, step, scale,
):
    fields, slots, points, _ = fields_ref.shape
    partners = partner_ids(me_ref[0], total, step)
    derivatives(
        lambda f, s: fields_ref[f, s], left_ref, right_ref, cols_ref, rows_ref, xi_ref, eta_ref, fields, slots, points
    )
    jumps(own_ref, (in0, in1, in2, in3), table_ref, jump_ref, conn_ref, me_ref[0], partners, points, scale)
    turned_ref[...] = jump_columns(jump_ref, scr_ref, fields, slots, points)
    for s in range(slots):
        for c in range(points // CHUNK):
            rows = pl.ds(c * CHUNK, CHUNK)
            parts = assemble(s, rows, density_ref, moduli_ref, diag_ref, cross_ref, xi_ref, eta_ref)
            for f in range(fields):
                rate_ref[f, s, rows, :] = parts[f] + column_part(turned_ref[rows, :], 2 * (s * fields + f), points)
        for f in range(fields):
            for side, row in ((0, 0), (1, points - 1)):
                line = rate_ref[f, s, pl.ds(row, 1), :] + jump_ref[4 * s + side, pl.ds(f, 1), :]
                rate_ref[f, s, pl.ds(row, 1), :] = line
                mine_ref[4 * s + side, pl.ds(f, 1), :] = line
    extract_lines(lambda f, s: rate_ref[f, s], mine_ref, scr_ref, fields, slots, points)
    fill_outboxes(mine_ref, (out0, out1, out2, out3), conn_ref, partners)


def second_kernel(
    fields_ref, rate_ref, density_ref, moduli_ref, diag_ref, cross_ref, left_ref, right_ref, peaks_ref, count_ref,
    new_ref, step_ref, cols_ref, rows_ref, xi_ref, eta_ref,
):
    fields, slots, points, _ = fields_ref.shape
    derivatives(
        lambda f, s: rate_ref[f, s], left_ref, right_ref, cols_ref, rows_ref, xi_ref, eta_ref, fields, slots, points
    )
    bound = jnp.max(peaks_ref[...], axis=0, keepdims=True)
    bound = jnp.max(bound, axis=1, keepdims=True)
    dt = CFL / (bound * (points - 1))
    half = 0.5 * dt * dt
    step_ref[...] = jnp.broadcast_to(half, step_ref.shape)
    for s in range(slots):
        live = s < count_ref[0]
        for c in range(points // CHUNK):
            rows = pl.ds(c * CHUNK, CHUNK)
            parts = assemble(s, rows, density_ref, moduli_ref, diag_ref, cross_ref, xi_ref, eta_ref)
            for f in range(fields):
                value = fields_ref[f, s, rows, :] + dt * rate_ref[f, s, rows, :] + half * parts[f]
                new_ref[f, s, rows, :] = jnp.where(live, value, 0.0)


def last_kernel(
    new_ref, half_ref, mine_ref, in0, in1, in2, in3, conn_ref, me_ref,
    final_ref, table_ref, jump_ref, scr_ref, turned_ref, *, total, step, scale,
):
    fields, slots, points, _ = new_ref.shape
    partners = partner_ids(me_ref[0], total, step)
    jumps(mine_ref, (in0, in1, in2, in3), table_ref, jump_ref, conn_ref, me_ref[0], partners, points, scale)
    for i in range(4 * slots):
        jump_ref[i] = jump_ref[i] * half_ref[...]
    turned_ref[...] = jump_columns(jump_ref, scr_ref, fields, slots, points)
    for s in range(slots):
        for f in range(fields):
            at = 2 * (s * fields + f)
            final_ref[f, s] = new_ref[f, s] + column_part(turned_ref[...], at, points)
            for side, row in ((0, 0), (1, points - 1)):
                line = final_ref[f, s, pl.ds(row, 1), :] + jump_ref[4 * s + side, pl.ds(f, 1), :]
                final_ref[f, s, pl.ds(row, 1), :] = line


def shards(fields, density, moduli, diag, cross, fc_extension, patch_count, connectivity):
    components, slots, points, _ = fields.shape
    total = lax.axis_size(PATCH_SUB)
    step = total // 2 + 1
    scale = PENALTY * (points - 1)
    sides = 4 * slots
    me = lax.axis_index(PATCH_SUB).reshape(1)
    inner, outer = fourier_matrix(points, fc_extension.shape[0])
    routes = swap_routes(total, step)

    box = jax.ShapeDtypeStruct((2, 8, points), F32)
    lines = jax.ShapeDtypeStruct((sides, 8, points), F32)
    grid = jax.ShapeDtypeStruct(fields.shape, F32)
    pair = jax.ShapeDtypeStruct((2 * points, 2 * points), BF16)
    square = pltpu.VMEM((points, points), F32)
    table = pltpu.VMEM((2 * sides, 8, points), F32)
    jump = pltpu.VMEM((sides, 8, points), F32)
    work = [
        pltpu.VMEM((components, 2 * points, 2 * points), BF16),
        pltpu.VMEM((components, 2 * points, 2 * points), BF16),
        pltpu.VMEM(fields.shape, F32),
        pltpu.VMEM(fields.shape, F32),
    ]

    def exchange(boxes):
        return [lax.ppermute(b, PATCH_SUB, r) for b, r in zip(boxes, routes)]

    *boxes, own, peak = pl.pallas_call(
        functools.partial(lines_kernel, total=total, step=step),
        out_shape=[box] * 4 + [lines, jax.ShapeDtypeStruct((total, points), F32)],
        in_specs=[VMEM] * 5 + [SMEM] * 3,
        out_specs=[VMEM] * 6,
        scratch_shapes=[square],
        compiler_params=PARAMS,
        name="lines",
    )(fields, density, moduli, diag, cross, connectivity, patch_count, me)
    arrived = exchange(boxes)
    peaks = lax.all_to_all(peak, PATCH_SUB, 0, 0, tiled=True)
    left, right = pl.pallas_call(
        matrix_kernel, out_shape=[pair, pair], in_specs=[VMEM] * 3, out_specs=[VMEM] * 2,
        compiler_params=PARAMS, name="matrix"
    )(jnp.asarray(inner), jnp.asarray(outer), fc_extension)
    rate, *boxes, mine = pl.pallas_call(
        functools.partial(first_kernel, total=total, step=step, scale=scale),
        out_shape=[grid] + [box] * 4 + [lines],
        in_specs=[VMEM] * 12 + [SMEM] * 2,
        out_specs=[VMEM] * 6,
        scratch_shapes=[table, jump, square, square] + work,
        compiler_params=PARAMS,
        name="first",
    )(fields, density, moduli, diag, cross, left, right, own, *arrived, connectivity, me)
    arrived = exchange(boxes)
    new, half = pl.pallas_call(
        second_kernel,
        out_shape=[grid, jax.ShapeDtypeStruct((8, points), F32)],
        in_specs=[VMEM] * 9 + [SMEM],
        out_specs=[VMEM] * 2,
        scratch_shapes=work,
        compiler_params=PARAMS,
        name="second",
    )(fields, rate, density, moduli, diag, cross, left, right, peaks, patch_count)
    return pl.pallas_call(
        functools.partial(last_kernel, total=total, step=step, scale=scale),
        out_shape=grid,
        in_specs=[VMEM] * 7 + [SMEM] * 2,
        out_specs=VMEM,
        scratch_shapes=[table, jump, square, square],
        compiler_params=PARAMS,
        name="last",
    )(new, half, mine, *arrived, connectivity, me)


def solution(mesh):
    torus = Mesh(
        mesh.devices.reshape(4, 8, 4, mesh.shape["sub"]), ("patch_0", "patch_1", "patch_2", "sub")
    )
    return jax.shard_map(
        shards,
        mesh=torus,
        in_specs=(
            P(None, PATCH_SUB, None, None),
            P(PATCH_SUB, None, None),
            P(None, PATCH_SUB, None, None),
            P(None, PATCH_SUB, None, None),
            P(None, PATCH_SUB, None, None),
            P(),
            P(PATCH_SUB),
            P(PATCH_SUB, None),
        ),
        out_specs=P(None, PATCH_SUB, None, None),
        check_vma=False,
    )
```

time: 165 us -> 52.7 us (0.32)
  other arithmetic: 55.8 us -> 0 us
  blocking collectives: 36 us -> 0 us
  local copies, waits for them, and re-layouts: 37.3 us -> 5.06 us
  Pallas kernels: 0 us -> 6.4 us
  starting transfers between devices: 25.8 us -> 31.8 us
  waiting for transfers between devices: 3.96 us -> 7.87 us
  matrix products: 3.13 us -> 0 us
    reduce_sum x2 -> x0, other arithmetic: 49.7 us -> none  [the longest x1 49.5 us: derivative_matrix(): jnp.sum(weights[:, None, None] * jnp.sin(angles), axis=0)]
    pmax x4 -> x0, blocking collectives: 36 us -> none  [over_axes(): return functools.reduce(lax.pmax, axes, x)]
    scatter-add x10 -> x0, local copies, waits for them, and re-layouts: 19.2 us -> none  [the longest x2 10.2 us: assemble(): rate = rate.at[:, :, :, points - 1].add(jump[3])]
    all_to_all x0 -> x1, starting transfers between devices: none -> 14.6 us  [shards(): peaks = lax.all_to_all(peak, PATCH_SUB, 0, 0, tiled=True)]
    ppermute x8, starting transfers between devices: 25.8 us -> 17.2 us  [exchange(): return [lax.ppermute(b, PATCH_SUB, r) for b, r in zip(boxes, routes)]]
    pallas_call x0 -> x5, Pallas kernels: none -> 6.4 us  [the longest x1 1.97 us: shards(): pl.pallas_call(functools.partial(last_kernel, total=total, step=step, sca...]
    scatter x8 -> x0, local copies, waits for them, and re-layouts: 5.91 us -> none  [partner_lines(): outbox = jnp.zeros((slot_count,) + line_shape, jnp.float32).at[target].se...]
    gather x10 -> x0, local copies, waits for them, and re-layouts: 5.67 us -> none  [the longest x8 4.44 us: partner_lines(): arrived[jnp.minimum(recv_pos, slot_count - 1)]]
  transfers between devices with their start and end apart: 8 -> 9, of which waited for: 1 -> 4; matrix products, arithmetic and copies ran while one was open for 39% -> 0% of each run, Pallas kernels for 0% -> 5%
where the time goes in v1:
time: 52.7 us; the launch traced here: 51.9 us
  starting transfers between devices  31.8 us (60%)
  waiting for transfers between devices  7.87 us (15%)
  Pallas kernels  6.4 us (12%)
  local copies, waits for them, and re-layouts  5.06 us (10%)
  between operations  0.79 us (1%)
    ppermute x8, starting transfers between devices, exchange(): return [lax.ppermute(b, PATCH_SUB, r) for b, r in zip(boxes, routes)]  17.2 us
    all_to_all x1, starting transfers between devices, shards(): peaks = lax.all_to_all(peak, PATCH_SUB, 0, 0, tiled=True)  14.6 us
    ppermute x8, waiting for transfers between devices, exchange(): return [lax.ppermute(b, PATCH_SUB, r) for b, r in zip(boxes, routes)]  7.86 us
    unnamed x30, local copies, waits for them, and re-layouts  5.06 us
    pallas_call x1, Pallas kernels, shards(): pl.pallas_call(functools.partial(last_kernel, total=total, step=step, sca...  1.97 us
    pallas_call x1, Pallas kernels, shards(): pl.pallas_call(functools.partial(lines_kernel, total=total, step=step), o...  1.66 us
    pallas_call x1, Pallas kernels, shards(): pl.pallas_call(functools.partial(first_kernel, total=total, step=step, sc...  1.56 us
  transfers between devices with their start and end apart: 9, of which 4 were waited for; matrix products, arithmetic and copies ran while one was open for 0% of the time, Pallas kernels for 5%

profile of v1, /device:TPU:8, one launch (start us, length us, event | category | flops | bytes accessed | tf_op | source)
XLA Modules:
  0.0 51.9 jit_solution(873510982534903756)
XLA Ops:
  0.7 0.0 copy-done.13
  0.7 0.1 copy.16.conn_ref
  0.8 1.1 %copy-done = f32[5,2,128,128]{3,2,1,0:T(8,128)S(1)} copy-done((f32[5,2,128,128]{3,2,1,0:T(8,128)S(1)}, f32[5,2,128,128]{3,2,1,0:T(8,128)}, u32[]{:S(2)}) %copy-start) | copy-done | bytes 655384
  1.9 0.9 %copy-done.2 = f32[2,2,128,128]{3,2,1,0:T(8,128)S(1)} copy-done((f32[2,2,128,128]{3,2,1,0:T(8,128)S(1)}, f32[2,2,128,128]{3,2,1,0:T(8,128)}, u32[]{:S(2)}) %copy-start.2) | copy-done | bytes 262168
  2.8 0.9 %copy-done.4 = f32[2,2,128,128]{3,2,1,0:T(8,128)S(1)} copy-done((f32[2,2,128,128]{3,2,1,0:T(8,128)S(1)}, f32[2,2,128,128]{3,2,1,0:T(8,128)}, u32[]{:S(2)}) %copy-start.4) | copy-done | bytes 262168
  3.8 0.9 %copy-done.6 = f32[2,2,128,128]{3,2,1,0:T(8,128)S(1)} copy-done((f32[2,2,128,128]{3,2,1,0:T(8,128)S(1)}, f32[2,2,128,128]{3,2,1,0:T(8,128)}, u32[]{:S(2)}) %copy-start.6) | copy-done | bytes 262168
  4.7 0.9 %copy-done.8 = f32[2,128,128]{2,1,0:T(8,128)S(1)} copy-done((f32[2,128,128]{2,1,0:T(8,128)S(1)}, f32[2,128,128]{2,1,0:T(8,128)}, u32[]{:S(2)}) %copy-start.8) | copy-done | bytes 131096
  5.6 1.7 %lines.1 = (f32[2,8,128]{2,1,0:T(8,128)S(1)}, f32[2,8,128]{2,1,0:T(8,128)S(1)}, f32[2,8,128]{2,1,0:T(8,128)S(1)}, f32[2,8,128]{2,1,0:T(8,128)S(1)}, f32[8,8,128]{2,1,0:T(8,128)S(1)}, /*index=5*/f32[256,128]{1,0:T(8,128)}) custom-call(f32[5,2,128,128]{3,2,1,0:T(8,128)S(1)} %copy-done, f32[2,128,128]{2,1,0:T(8,128)S(1)} %copy-done.8, ...), custom_call_target="tpu_custom_call" | custom-call | tf_op jit(solution)/shard_map/lines/pallas_call | solution.py:331
  7.3 14.6 %all-to-all-start = ((f32[256,1,128]{2,1,0:T(1,128)}), f32[256,1,128]{2,1,0:T(1,128)S(1)}, u32[]{:S(2)}, u32[]{:S(2)}) async-start(f32[256,1,128]{2,1,0:T(1,128)} %bitcast.2), calls=%async_computation | async-start | bytes 262144 | tf_op jit(solution)/shard_map/all_to_all | solution.py:341
  21.9 0.2 collective-permute-start
  22.1 6.6 %collective-permute-start.1 = (f32[2,8,128]{2,1,0:T(8,128)S(1)}, f32[2,8,128]{2,1,0:T(8,128)S(1)}, u32[]{:S(2)}, u32[]{:S(2)}) collective-permute-start(f32[2,8,128]{2,1,0:T(8,128)S(1)} %get-tuple-element.25), channel_id=1, source_target_pairs={{0,255},{1,2},{2,1},{3,4},{4,3},{5,6},{6,5},{7,8},{8,7},{9,10},{10... | collective-permute-start | bytes 24584 | tf_op jit(solution)/shard_map/ppermute | solution.py:329
  28.7 2.0 %collective-permute-start.3 = (f32[2,8,128]{2,1,0:T(8,128)S(1)}, f32[2,8,128]{2,1,0:T(8,128)S(1)}, u32[]{:S(2)}, u32[]{:S(2)}) collective-permute-start(f32[2,8,128]{2,1,0:T(8,128)S(1)} %get-tuple-element.27), channel_id=1, source_target_pairs={{0,127},{1,130},{2,129},{3,132},{4,131},{5,134},{6,133},{7,136},{8... | collective-permute-start | bytes 24584 | tf_op jit(solution)/shard_map/ppermute | solution.py:329
  30.7 0.1 copy.15.ext_ref
  30.8 0.4 matrix.1
  31.3 2.0 %collective-permute-done.2.in2 = f32[2,8,128]{2,1,0:T(8,128)S(1)} collective-permute-done((f32[2,8,128]{2,1,0:T(8,128)S(1)}, f32[2,8,128]{2,1,0:T(8,128)S(1)}, u32[]{:S(2)}, u32[]{:S(2)}) %collective-permute-start.2) | collective-permute-done | bytes 8224 | tf_op jit(solution)/shard_map/ppermute | solution.py:329
  33.3 2.7 %collective-permute-done.3.in3 = f32[2,8,128]{2,1,0:T(8,128)S(1)} collective-permute-done((f32[2,8,128]{2,1,0:T(8,128)S(1)}, f32[2,8,128]{2,1,0:T(8,128)S(1)}, u32[]{:S(2)}, u32[]{:S(2)}) %collective-permute-start.3) | collective-permute-done | bytes 8224 | tf_op jit(solution)/shard_map/ppermute | solution.py:329
  36.0 1.6 %first.1 = (f32[5,2,128,128]{3,2,1,0:T(8,128)S(1)}, f32[2,8,128]{2,1,0:T(8,128)S(1)}, f32[2,8,128]{2,1,0:T(8,128)S(1)}, f32[2,8,128]{2,1,0:T(8,128)S(1)}, f32[2,...) custom-call(f32[5,2,128,128]{3,2,1,0:T(8,128)S(1)} %copy-done.1, f32[2,128,128]{2,1,0:T(8,128)S(1)} %copy-done.9, ...), custom_call_target="tpu_custom_call" | custom-call | tf_op jit(solution)/shard_map/first/pallas_call | solution.py:346
  37.6 1.0 %collective-permute-start.4 = (f32[2,8,128]{2,1,0:T(8,128)S(1)}, f32[2,8,128]{2,1,0:T(8,128)S(1)}, u32[]{:S(2)}, u32[]{:S(2)}) collective-permute-start(f32[2,8,128]{2,1,0:T(8,128)S(1)} %get-tuple-element.33), channel_id=1, source_target_pairs={{0,1},{1,0},{2,3},{3,2},{4,5},{5,4},{6,7},{7,6},{8,9},{9,8},{10,11... | collective-permute-start | bytes 24584 | tf_op jit(solution)/shard_map/ppermute | solution.py:329
  38.5 4.1 %collective-permute-start.5 = (f32[2,8,128]{2,1,0:T(8,128)S(1)}, f32[2,8,128]{2,1,0:T(8,128)S(1)}, u32[]{:S(2)}, u32[]{:S(2)}) collective-permute-start(f32[2,8,128]{2,1,0:T(8,128)S(1)} %get-tuple-element.34), channel_id=1, source_target_pairs={{0,255},{1,2},{2,1},{3,4},{4,3},{5,6},{6,5},{7,8},{8,7},{9,10},{10... | collective-permute-start | bytes 24584 | tf_op jit(solution)/shard_map/ppermute | solution.py:329
  42.6 3.3 %collective-permute-start.7 = (f32[2,8,128]{2,1,0:T(8,128)S(1)}, f32[2,8,128]{2,1,0:T(8,128)S(1)}, u32[]{:S(2)}, u32[]{:S(2)}) collective-permute-start(f32[2,8,128]{2,1,0:T(8,128)S(1)} %get-tuple-element.36), channel_id=1, source_target_pairs={{0,127},{1,130},{2,129},{3,132},{4,131},{5,134},{6,133},{7,136},{8... | collective-permute-start | bytes 24584 | tf_op jit(solution)/shard_map/ppermute | solution.py:329
  46.0 0.8 %second.1 = (f32[5,2,128,128]{3,2,1,0:T(8,128)S(1)}, f32[8,128]{1,0:T(8,128)S(1)}) custom-call(f32[5,2,128,128]{3,2,1,0:T(8,128)S(1)} %copy-done.1, f32[5,2,128,128]{3,2,1,0:T(8,128)S(1)} %get-tuple-element.28.rate_ref, f32[2,128,128]{2,1,0:T(8,128)S(1)} %copy-done.9, f32[2,2,128,128]{3,2,1,0:T(8,128)S(1)} %copy-done.3, f32[2,2,128,128]{3,2,1,0:T(8,128)S(1)} %copy-done.5, ...), custom_call_target="tpu_custom_call" | custom-call | tf_op jit(solution)/shard_map/second/pallas_call | solution.py:356
  46.8 0.4 collective-permute-done.6.in2
  47.2 2.7 %collective-permute-done.7.in3 = f32[2,8,128]{2,1,0:T(8,128)S(1)} collective-permute-done((f32[2,8,128]{2,1,0:T(8,128)S(1)}, f32[2,8,128]{2,1,0:T(8,128)S(1)}, u32[]{:S(2)}, u32[]{:S(2)}) %collective-permute-start.7) | collective-permute-done | bytes 8224 | tf_op jit(solution)/shard_map/ppermute | solution.py:329
  49.9 2.0 %last.1 = f32[5,2,128,128]{3,2,1,0:T(8,128)} custom-call(f32[5,2,128,128]{3,2,1,0:T(8,128)S(1)} %get-tuple-element.30.new_ref, f32[8,128]{1,0:T(8,128)S(1)} %get-tuple-element.31.half_ref, f32[8,8,128]{2,1,0:T(8,128)S(1)} %get-tuple-element.32.mine_ref, f32[2,8,128]{2,1,0:T(8,128)S(1)} %collective-permute-done.4.in0, ...), custom_call_target="tpu_custom_call" | custom-call | tf_op jit(solution)/shard_map/last/pallas_call | solution.py:365
  (29 shorter events, 0.1 us)
Async XLA Ops:
  0.0 0.7 %copy-start.13 = (s32[8,3]{0,1:T(4,128)S(1)}, s32[8,3]{0,1:T(4,128)}, u32[]{:S(2)}) copy-start(s32[8,3]{0,1:T(4,128)} %param.17) | copy-start | bytes 292
  0.8 1.1 %copy-start = (f32[5,2,128,128]{3,2,1,0:T(8,128)S(1)}, f32[5,2,128,128]{3,2,1,0:T(8,128)}, u32[]{:S(2)}) copy-start(f32[5,2,128,128]{3,2,1,0:T(8,128)} %fields_ref.5) | copy-start | bytes 1966084
  1.9 0.9 %copy-start.2 = (f32[2,2,128,128]{3,2,1,0:T(8,128)S(1)}, f32[2,2,128,128]{3,2,1,0:T(8,128)}, u32[]{:S(2)}) copy-start(f32[2,2,128,128]{3,2,1,0:T(8,128)} %moduli_ref.5) | copy-start | bytes 786436
  2.8 0.9 %copy-start.4 = (f32[2,2,128,128]{3,2,1,0:T(8,128)S(1)}, f32[2,2,128,128]{3,2,1,0:T(8,128)}, u32[]{:S(2)}) copy-start(f32[2,2,128,128]{3,2,1,0:T(8,128)} %diag_ref.5) | copy-start | bytes 786436
  3.8 0.9 %copy-start.6 = (f32[2,2,128,128]{3,2,1,0:T(8,128)S(1)}, f32[2,2,128,128]{3,2,1,0:T(8,128)}, u32[]{:S(2)}) copy-start(f32[2,2,128,128]{3,2,1,0:T(8,128)} %cross_ref.5) | copy-start | bytes 786436
  4.7 0.9 %copy-start.8 = (f32[2,128,128]{2,1,0:T(8,128)S(1)}, f32[2,128,128]{2,1,0:T(8,128)}, u32[]{:S(2)}) copy-start(f32[2,128,128]{2,1,0:T(8,128)} %density_ref.5) | copy-start | bytes 393220
  5.6 25.2 %copy-start.10 = (f32[128,25]{1,0:T(8,128)S(1)}, f32[128,25]{1,0:T(8,128)}, u32[]{:S(2)}) copy-start(f32[128,25]{1,0:T(8,128)} %constant.27.clone.outer_ref) | copy-start | bytes 38404
  5.6 25.2 %copy-start.11 = (f32[128,128]{1,0:T(8,128)S(1)}, f32[128,128]{1,0:T(8,128)}, u32[]{:S(2)}) copy-start(f32[128,128]{1,0:T(8,128)} %constant.26.clone.inner_ref) | copy-start | bytes 196612
  5.6 30.4 %copy-start.1 = (f32[5,2,128,128]{3,2,1,0:T(8,128)S(1)}, f32[5,2,128,128]{3,2,1,0:T(8,128)}, u32[]{:S(2)}) copy-start(f32[5,2,128,128]{3,2,1,0:T(8,128)} %fields_ref.5) | copy-start | bytes 1966084
  5.6 30.4 %copy-start.5 = (f32[2,2,128,128]{3,2,1,0:T(8,128)S(1)}, f32[2,2,128,128]{3,2,1,0:T(8,128)}, u32[]{:S(2)}) copy-start(f32[2,2,128,128]{3,2,1,0:T(8,128)} %diag_ref.5) | copy-start | bytes 786436
  5.6 30.4 %copy-start.7 = (f32[2,2,128,128]{3,2,1,0:T(8,128)S(1)}, f32[2,2,128,128]{3,2,1,0:T(8,128)}, u32[]{:S(2)}) copy-start(f32[2,2,128,128]{3,2,1,0:T(8,128)} %cross_ref.5) | copy-start | bytes 786436
  7.3 28.7 %copy-start.3 = (f32[2,2,128,128]{3,2,1,0:T(8,128)S(1)}, f32[2,2,128,128]{3,2,1,0:T(8,128)}, u32[]{:S(2)}) copy-start(f32[2,2,128,128]{3,2,1,0:T(8,128)} %moduli_ref.5) | copy-start | bytes 786436
  7.3 23.4 %copy-start.12 = (f32[25,10]{0,1:T(8,128)S(1)}, f32[25,10]{0,1:T(8,128)}, u32[]{:S(2)}) copy-start(f32[25,10]{0,1:T(8,128)} %param.15) | copy-start | bytes 3004
  7.3 38.7 %all-to-all-start = ((f32[256,1,128]{2,1,0:T(1,128)}), f32[256,1,128]{2,1,0:T(1,128)S(1)}, u32[]{:S(2)}, u32[]{:S(2)}) async-start(f32[256,1,128]{2,1,0:T(1,128)} %bitcast.2), calls=%async_computation | async-start | bytes 262144 | tf_op jit(solution)/shard_map/all_to_all | solution.py:341
  21.9 14.1 %copy-start.9 = (f32[2,128,128]{2,1,0:T(8,128)S(1)}, f32[2,128,128]{2,1,0:T(8,128)}, u32[]{:S(2)}) copy-start(f32[2,128,128]{2,1,0:T(8,128)} %density_ref.5) | copy-start | bytes 393220
  21.9 9.4 %collective-permute-start = (f32[2,8,128]{2,1,0:T(8,128)S(1)}, f32[2,8,128]{2,1,0:T(8,128)S(1)}, u32[]{:S(2)}, u32[]{:S(2)}) collective-permute-start(f32[2,8,128]{2,1,0:T(8,128)S(1)} %get-tuple-element.24), channel_id=1, source_target_pairs={{0,1},{1,0},{2,3},{3,2},{4,5},{5,4},{6,7},{7,6},{8,9},{9,8},{10,11... | collective-permute-start | bytes 24584 | tf_op jit(solution)/shard_map/ppermute | solution.py:329
  22.1 9.2 %collective-permute-start.1 = (f32[2,8,128]{2,1,0:T(8,128)S(1)}, f32[2,8,128]{2,1,0:T(8,128)S(1)}, u32[]{:S(2)}, u32[]{:S(2)}) collective-permute-start(f32[2,8,128]{2,1,0:T(8,128)S(1)} %get-tuple-element.25), channel_id=1, source_target_pairs={{0,255},{1,2},{2,1},{3,4},{4,3},{5,6},{6,5},{7,8},{8,7},{9,10},{10... | collective-permute-start | bytes 24584 | tf_op jit(solution)/shard_map/ppermute | solution.py:329
  28.7 4.6 %collective-permute-start.2 = (f32[2,8,128]{2,1,0:T(8,128)S(1)}, f32[2,8,128]{2,1,0:T(8,128)S(1)}, u32[]{:S(2)}, u32[]{:S(2)}) collective-permute-start(f32[2,8,128]{2,1,0:T(8,128)S(1)} %get-tuple-element.26), channel_id=1, source_target_pairs={{0,129},{1,128},{2,131},{3,130},{4,133},{5,132},{6,135},{7,134},{8... | collective-permute-start | bytes 24584 | tf_op jit(solution)/shard_map/ppermute | solution.py:329
  28.7 7.3 %collective-permute-start.3 = (f32[2,8,128]{2,1,0:T(8,128)S(1)}, f32[2,8,128]{2,1,0:T(8,128)S(1)}, u32[]{:S(2)}, u32[]{:S(2)}) collective-permute-start(f32[2,8,128]{2,1,0:T(8,128)S(1)} %get-tuple-element.27), channel_id=1, source_target_pairs={{0,127},{1,130},{2,129},{3,132},{4,131},{5,134},{6,133},{7,136},{8... | collective-permute-start | bytes 24584 | tf_op jit(solution)/shard_map/ppermute | solution.py:329
  37.6 9.2 %collective-permute-start.4 = (f32[2,8,128]{2,1,0:T(8,128)S(1)}, f32[2,8,128]{2,1,0:T(8,128)S(1)}, u32[]{:S(2)}, u32[]{:S(2)}) collective-permute-start(f32[2,8,128]{2,1,0:T(8,128)S(1)} %get-tuple-element.33), channel_id=1, source_target_pairs={{0,1},{1,0},{2,3},{3,2},{4,5},{5,4},{6,7},{7,6},{8,9},{9,8},{10,11... | collective-permute-start | bytes 24584 | tf_op jit(solution)/shard_map/ppermute | solution.py:329
  38.5 8.2 %collective-permute-start.5 = (f32[2,8,128]{2,1,0:T(8,128)S(1)}, f32[2,8,128]{2,1,0:T(8,128)S(1)}, u32[]{:S(2)}, u32[]{:S(2)}) collective-permute-start(f32[2,8,128]{2,1,0:T(8,128)S(1)} %get-tuple-element.34), channel_id=1, source_target_pairs={{0,255},{1,2},{2,1},{3,4},{4,3},{5,6},{6,5},{7,8},{8,7},{9,10},{10... | collective-permute-start | bytes 24584 | tf_op jit(solution)/shard_map/ppermute | solution.py:329
  42.6 4.6 %collective-permute-start.6 = (f32[2,8,128]{2,1,0:T(8,128)S(1)}, f32[2,8,128]{2,1,0:T(8,128)S(1)}, u32[]{:S(2)}, u32[]{:S(2)}) collective-permute-start(f32[2,8,128]{2,1,0:T(8,128)S(1)} %get-tuple-element.35), channel_id=1, source_target_pairs={{0,129},{1,128},{2,131},{3,130},{4,133},{5,132},{6,135},{7,134},{8... | collective-permute-start | bytes 24584 | tf_op jit(solution)/shard_map/ppermute | solution.py:329
  42.6 7.3 %collective-permute-start.7 = (f32[2,8,128]{2,1,0:T(8,128)S(1)}, f32[2,8,128]{2,1,0:T(8,128)S(1)}, u32[]{:S(2)}, u32[]{:S(2)}) collective-permute-start(f32[2,8,128]{2,1,0:T(8,128)S(1)} %get-tuple-element.36), channel_id=1, source_target_pairs={{0,127},{1,130},{2,129},{3,132},{4,131},{5,134},{6,133},{7,136},{8... | collective-permute-start | bytes 24584 | tf_op jit(solution)/shard_map/ppermute | solution.py:329

commit v2 on v0

v2 whole, which is shorter than its diff:
```python
import functools

import jax
import jax.numpy as jnp
import numpy as np
from jax import lax
from jax.experimental import pallas as pl
from jax.experimental.pallas import tpu as pltpu
from jax.sharding import Mesh
from jax.sharding import PartitionSpec as P

PATCH_SUB = ("patch_0", "patch_1", "patch_2", "sub")

CFL = 0.5
PENALTY = 0.5
CHUNK = 16
F32 = jnp.float32
BF16 = jnp.bfloat16
VMEM = pl.BlockSpec(memory_space=pltpu.VMEM)
SMEM = pl.BlockSpec(memory_space=pltpu.SMEM)
ANY = pl.BlockSpec(memory_space=pltpu.HBM)
PARAMS = pltpu.CompilerParams(vmem_limit_bytes=14 * 1024 * 1024)
CONN_LANE = 40
PEAK_LANE = 64


def fourier_matrix(points, cont):
    length = points + cont
    delta = np.arange(points)[:, None] - np.arange(length)[None, :]
    safe = np.where(delta == 0, 1, delta)
    scale = np.pi * (points - 1) / length
    sign = np.where(delta % 2 == 0, 1.0, -1.0)
    full = np.where(delta == 0, 0.0, scale * sign / np.sin(np.pi * safe / length))
    return full[:, :points].astype(np.float32), full[:, points:].astype(np.float32)


def offsets(total):
    step = total // 2 + 1
    return (1, -1, step, -step)


def lane_ids(shape):
    return lax.broadcasted_iota(jnp.int32, shape, len(shape) - 1)


def split(value):
    high = value.astype(BF16)
    return high, (value - high.astype(F32)).astype(BF16)


def boundary_columns(load, scr_ref, fields, slots, points):
    lanes = lane_ids((points, points))
    columns = jnp.zeros((points, points), F32)
    for s in range(slots):
        for f in range(fields):
            at = 2 * (s * fields + f)
            columns = jnp.where((lanes == at) | (lanes == at + 1), pltpu.roll(load(f, s), at + 1, 1), columns)
    scr_ref[...] = columns.T


def boundary_lines(ref, own_ref, row, scr_ref, fields, slots, points):
    boundary_columns(lambda f, s: ref[f, s], scr_ref, fields, slots, points)
    for s in range(slots):
        for f in range(fields):
            own_ref[4 * s, pl.ds(row + f, 1), :] = ref[f, s, pl.ds(0, 1), :]
            own_ref[4 * s + 1, pl.ds(row + f, 1), :] = ref[f, s, pl.ds(points - 1, 1), :]
        base = 2 * s * fields
        own_ref[4 * s + 2, pl.ds(row, fields), :] = scr_ref[pl.ds(base + 1, fields, stride=2), :]
        own_ref[4 * s + 3, pl.ds(row, fields), :] = scr_ref[pl.ds(base, fields, stride=2), :]


def column_part(turned, at, points):
    moved = pltpu.roll(turned, points - 1 - at, 1)
    lanes = lane_ids(moved.shape)
    return jnp.where((lanes == 0) | (lanes == points - 1), moved, 0.0)


def turn_jumps(jump_ref, scr_ref, fields, slots):
    for s in range(slots):
        for f in range(fields):
            at = 2 * (s * fields + f)
            scr_ref[pl.ds(at + 1, 1), :] = jump_ref[4 * s + 2, pl.ds(f, 1), :]
            scr_ref[pl.ds(at, 1), :] = jump_ref[4 * s + 3, pl.ds(f, 1), :]
    return scr_ref[...].T


def derivatives(f, value_of, left_ref, right_ref, cols_ref, rows_ref, xi_ref, eta_ref, slots, points):
    for s in range(slots):
        high, low = split(value_of(s))
        cols_ref[f, pl.ds(0, points), pl.ds(s * points, points)] = high
        cols_ref[f, pl.ds(points, points), pl.ds(s * points, points)] = low
        rows_ref[f, pl.ds(s * points, points), pl.ds(0, points)] = high
        rows_ref[f, pl.ds(s * points, points), pl.ds(points, points)] = low
    got = jnp.dot(left_ref[...], cols_ref[f], preferred_element_type=F32)
    along = got[:points] + got[points:]
    for s in range(slots):
        xi_ref[f, s] = along[:, s * points : (s + 1) * points]
    got = jnp.dot(rows_ref[f], right_ref[...], preferred_element_type=F32)
    along = got[:, :points] + got[:, points:]
    for s in range(slots):
        eta_ref[f, s] = along[s * points : (s + 1) * points]


def assemble(s, rows, density_ref, moduli_ref, diag_ref, cross_ref, xi_ref, eta_ref):
    xi_x, eta_y = diag_ref[0, s, rows, :], diag_ref[1, s, rows, :]
    xi_y, eta_x = cross_ref[0, s, rows, :], cross_ref[1, s, rows, :]
    lame, shear = moduli_ref[0, s, rows, :], moduli_ref[1, s, rows, :]
    light = 1.0 / density_ref[s, rows, :]
    stiff = lame + 2.0 * shear

    def dx(f):
        return xi_x * xi_ref[f, s, rows, :] + eta_x * eta_ref[f, s, rows, :]

    def dy(f):
        return xi_y * xi_ref[f, s, rows, :] + eta_y * eta_ref[f, s, rows, :]

    one_x, two_y = dx(0), dy(1)
    return (
        (dx(2) + dy(4)) * light,
        (dx(4) + dy(3)) * light,
        stiff * one_x + lame * two_y,
        lame * one_x + stiff * two_y,
        shear * (dy(0) + dx(1)),
    )


def build_matrices(inner, outer, ext, left_ref, right_ref):
    points = inner.shape[0]
    match = ext.shape[0] // 2
    rows = lax.broadcasted_iota(jnp.int32, (2 * match, points), 0)
    lanes = lane_ids((2 * match, points))
    place = jnp.where(rows < match, points - match + rows, rows - match)
    spread = jnp.where(lanes == place, 1.0, 0.0).astype(F32)
    exact = dict(precision=lax.Precision.HIGHEST, preferred_element_type=F32)
    wide = lax.dot_general(ext, spread, (((0,), (0,)), ((), ())), **exact)
    full = inner + jnp.dot(outer, wide, **exact)
    zero = jnp.zeros((points, points), BF16)
    first, second = pl.ds(0, points), pl.ds(points, points)
    high, low = split(full)
    left_ref[first, first] = high
    left_ref[first, second] = high
    left_ref[second, first] = low
    left_ref[second, second] = zero
    high, low = split(full.T)
    right_ref[first, first] = high
    right_ref[second, first] = high
    right_ref[first, second] = low
    right_ref[second, second] = zero


def front_kernel(
    fields_in, density_in, moduli_in, diag_in, cross_in, inner_in, outer_in, ext_in, conn_ref, count_ref, me_ref,
    out0, out1, out2, out3, own_ref, card_ref, rate_ref, left_ref, right_ref,
    fields_ref, density_ref, moduli_ref, diag_ref, cross_ref,
    inner_ref, outer_ref, ext_ref, scr_ref, cols_ref, rows_ref, xi_ref, eta_ref, sems, *, total,
):
    fields, slots, points, _ = fields_ref.shape
    sides = 4 * slots

    def fetch(source, target, at):
        copy = pltpu.make_async_copy(source, target, sems.at[at])
        copy.start()
        return copy

    small = [fetch(a, b, i) for i, (a, b) in enumerate(((inner_in, inner_ref), (outer_in, outer_ref), (ext_in, ext_ref)))]
    large = [fetch(fields_in.at[f], fields_ref.at[f], 3 + f) for f in range(fields)]
    coefs = [
        fetch(a, b, 3 + fields + i)
        for i, (a, b) in enumerate(
            ((density_in, density_ref), (moduli_in, moduli_ref), (diag_in, diag_ref), (cross_in, cross_ref))
        )
    ]
    for copy in small:
        copy.wait()
    build_matrices(inner_ref[...], outer_ref[...], ext_ref[...], left_ref, right_ref)
    for f in range(fields):
        large[f].wait()
        derivatives(
            f, lambda s, f=f: fields_ref[f, s], left_ref, right_ref, cols_ref, rows_ref, xi_ref, eta_ref, slots, points
        )
    boundary_lines(fields_ref, own_ref, 0, scr_ref, fields, slots, points)
    for copy in coefs:
        copy.wait()

    peak = jnp.zeros((8, points), F32)
    for s in range(slots):
        live = s < count_ref[0]
        for c in range(points // CHUNK):
            rows = pl.ds(c * CHUNK, CHUNK)
            stiff = moduli_ref[0, s, rows, :] + 2.0 * moduli_ref[1, s, rows, :]
            xi_x, eta_y = diag_ref[0, s, rows, :], diag_ref[1, s, rows, :]
            xi_y, eta_x = cross_ref[0, s, rows, :], cross_ref[1, s, rows, :]
            speed = jnp.sqrt(stiff / density_ref[s, rows, :]) * (
                jnp.sqrt(xi_x * xi_x + xi_y * xi_y) + jnp.sqrt(eta_x * eta_x + eta_y * eta_y)
            )
            speed = jnp.where(live, speed, 0.0)
            for r in range(CHUNK // 8):
                peak = jnp.maximum(peak, speed[8 * r : 8 * r + 8])
            parts = assemble(s, rows, density_ref, moduli_ref, diag_ref, cross_ref, xi_ref, eta_ref)
            for f in range(fields):
                rate_ref[f, s, rows, :] = parts[f]
    peak = jnp.max(jnp.max(peak, axis=0, keepdims=True), axis=1, keepdims=True)
    boundary_lines(rate_ref, own_ref, 8, scr_ref, fields, slots, points)

    lanes = lane_ids((8, points))
    corners = jnp.zeros((8, points), F32)
    for s in range(slots):
        for a in range(2):
            k = 4 * s + 2 * a
            moved = pltpu.roll(own_ref[4 * s + a, pl.ds(0, 8), :], k + 1, 1)
            corners = jnp.where((lanes == k) | (lanes == k + 1), moved, corners)
    scr_ref[pl.ds(0, 8), :] = corners
    lane = lane_ids((1, points))
    card = jnp.where(lane == PEAK_LANE, peak, 0.0)
    for f in range(fields):
        moved = pltpu.roll(scr_ref[pl.ds(f, 1), :], 8 * f, 1)
        card = jnp.where((lane >= 8 * f) & (lane < 8 * f + sides), moved, card)
    for i in range(sides):
        for c in range(3):
            card = jnp.where(lane == CONN_LANE + 3 * i + c, conn_ref[c, i].astype(F32), card)
    card_ref[...] = jnp.broadcast_to(card, card_ref.shape)

    for offset, out_ref in zip(offsets(total), (out0, out1, out2, out3)):
        partner = lax.rem(me_ref[0] + offset + total, total)
        first = jnp.int32(0)
        second = jnp.int32(0)
        count = jnp.int32(0)
        for i in range(sides):
            match = conn_ref[0, i] == partner
            first = jnp.where(match & (count == 0), i, first)
            second = jnp.where(match & (count == 1), i, second)
            count = count + match.astype(jnp.int32)
        out_ref[0] = own_ref[first]
        out_ref[1] = own_ref[second]


def corner_terms(cards_ref, conn_ref, near_ref, total, sides, points):
    shape = (2 * sides, points)
    rows = lax.broadcasted_iota(jnp.int32, shape, 0)
    lanes = lane_ids(shape)
    steps = (0,) + offsets(total)
    owner = jnp.zeros(shape, jnp.int32)
    strip = jnp.zeros(shape, jnp.int32)
    flip = jnp.zeros(shape, jnp.int32)
    for i in range(sides):
        here = rows // 2 == i
        held = jnp.maximum(conn_ref[0, i], 0)
        owner = jnp.where(here, held, owner)
        strip = jnp.where(here, conn_ref[1, i], strip)
        flip = jnp.where(here, conn_ref[2, i], flip)
        for d, offset in enumerate(steps):
            card = cards_ref[pl.ds(lax.rem(held + offset + total, total), 1), :]
            near_ref[d, pl.ds(2 * i, 1), :] = card
            near_ref[d, pl.ds(2 * i + 1, 1), :] = card

    def pick(array, index):
        return jnp.take_along_axis(array, index, axis=1)

    side = strip % 4
    base = strip - side
    at_end = jnp.where(rows % 2 == 0, 1 - flip, flip)
    across = side < 2
    other = jnp.where(across, 2 + at_end, at_end)
    odd = side % 2
    first = jnp.where(across, odd, at_end)
    second = jnp.where(across, at_end, odd)
    spread = 8 * jnp.minimum(lanes, 4)
    partner = near_ref[0]
    value = pick(partner, spread + base + 2 * first + 1 - second)
    link = CONN_LANE + 3 * (base + other)
    far_owner = pick(partner, link).astype(jnp.int32)
    far_strip = pick(partner, link + 1).astype(jnp.int32)
    far_flip = pick(partner, link + 2).astype(jnp.int32)
    far_card = partner
    for d, offset in enumerate(steps):
        if d:
            far_card = jnp.where(far_owner == lax.rem(owner + offset + total, total), near_ref[d], far_card)
    far_side = far_strip % 4
    far_base = far_strip - far_side
    point = jnp.where(far_flip == 1, 1 - odd, odd)
    far_across = far_side < 2
    far_odd = far_side % 2
    far_first = jnp.where(far_across, far_odd, point)
    far_second = jnp.where(far_across, point, far_odd)
    beyond = pick(far_card, spread + far_base + 2 * far_first + 1 - far_second)
    return jnp.where(far_owner >= 0, beyond - value, 0.0)


def last_kernel(
    fields_ref, inside_ref, density_ref, moduli_ref, diag_ref, cross_ref, left_ref, right_ref, own_ref, cards_ref,
    in0, in1, in2, in3, conn_ref, count_ref, me_ref,
    final_out,
    table_ref, jump_ref, mine_ref, near_ref, scr_ref, turned_ref, corner_ref,
    cols_ref, rows_ref, xi_ref, eta_ref, rate_ref, final_ref, sems, *, total, scale,
):
    fields, slots, points, _ = fields_ref.shape
    sides = 4 * slots
    lanes = lane_ids((8, points))
    scr_ref[...] = jnp.zeros(scr_ref.shape, F32)

    for i in range(sides):
        table_ref[i] = own_ref[i]
    for k, in_ref in enumerate((in0, in1, in2, in3)):
        table_ref[sides + 2 * k] = in_ref[0]
        table_ref[sides + 2 * k + 1] = in_ref[1]
    weights = []
    partner_rates = []
    for i in range(sides):
        owner = conn_ref[0, i]
        strip = conn_ref[1, i]
        position = jnp.int32(0)
        for j in range(sides):
            if j != i:
                before = (conn_ref[0, j] == owner) & (conn_ref[1, j] < strip)
                position = position + before.astype(jnp.int32)
        place = strip
        for k, offset in enumerate(offsets(total)):
            source = lax.rem(me_ref[0] - offset + total, total)
            place = jnp.where(owner == source, sides + 2 * k + position, place)
        place = jnp.clip(place, 0, 2 * sides - 1)
        index = jnp.where(conn_ref[2, i] == 1, points - 1 - lanes, lanes)
        line = jnp.take_along_axis(table_ref[place, pl.ds(0, 8), :], index, axis=1)
        rate = jnp.take_along_axis(table_ref[place, pl.ds(8, 8), :], index, axis=1)
        weight = jnp.where(owner >= 0, scale, 0.0).astype(F32)
        jump = weight * (line - own_ref[i, pl.ds(0, 8), :])
        jump_ref[i] = jump
        weights.append(weight)
        partner_rates.append(rate - jump)
    turned_ref[...] = turn_jumps(jump_ref, scr_ref, fields, slots)

    for f in range(fields):
        for s in range(slots):
            rate_ref[f, s] = inside_ref[f, s] + column_part(turned_ref[...], 2 * (s * fields + f), points)
            for side, row in ((0, 0), (1, points - 1)):
                line = rate_ref[f, s, pl.ds(row, 1), :] + jump_ref[4 * s + side, pl.ds(f, 1), :]
                rate_ref[f, s, pl.ds(row, 1), :] = line
        derivatives(
            f, lambda s, f=f: rate_ref[f, s], left_ref, right_ref, cols_ref, rows_ref, xi_ref, eta_ref, slots, points
        )
    boundary_lines(rate_ref, mine_ref, 0, scr_ref, fields, slots, points)

    bound = jnp.max(cards_ref[...], axis=0, keepdims=True)
    bound = jnp.where(lane_ids(bound.shape) == PEAK_LANE, bound, 0.0)
    bound = jnp.max(bound, axis=1, keepdims=True)
    dt = CFL / (bound * (points - 1))
    half = 0.5 * dt * dt

    corner_ref[...] = jnp.zeros(corner_ref.shape, F32)
    corner_ref[pl.ds(0, 2 * sides), :] = corner_terms(cards_ref, conn_ref, near_ref, total, sides, points)
    corners = corner_ref[...].T[:8]
    for i in range(sides):
        partner = partner_rates[i] + scale * column_part(corners, 2 * i, points)
        jump_ref[i] = half * weights[i] * (partner - mine_ref[i])
    turned_ref[...] = turn_jumps(jump_ref, scr_ref, fields, slots)

    copies = []
    for s in range(slots):
        live = s < count_ref[0]
        for c in range(points // CHUNK):
            rows = pl.ds(c * CHUNK, CHUNK)
            parts = assemble(s, rows, density_ref, moduli_ref, diag_ref, cross_ref, xi_ref, eta_ref)
            for f in range(fields):
                value = fields_ref[f, s, rows, :] + dt * rate_ref[f, s, rows, :] + half * parts[f]
                value = value + column_part(turned_ref[rows, :], 2 * (s * fields + f), points)
                final_ref[f, s, rows, :] = jnp.where(live, value, 0.0)
        for f in range(fields):
            for side, row in ((0, 0), (1, points - 1)):
                line = final_ref[f, s, pl.ds(row, 1), :] + jump_ref[4 * s + side, pl.ds(f, 1), :]
                final_ref[f, s, pl.ds(row, 1), :] = jnp.where(live, line, 0.0)
            copy = pltpu.make_async_copy(final_ref.at[f, s], final_out.at[f, s], sems.at[s * fields + f])
            copy.start()
            copies.append(copy)
    for copy in copies:
        copy.wait()


def shards(fields, density, moduli, diag, cross, fc_extension, patch_count, connectivity):
    components, slots, points, _ = fields.shape
    total = lax.axis_size(PATCH_SUB)
    scale = PENALTY * (points - 1)
    sides = 4 * slots
    me = lax.axis_index(PATCH_SUB).reshape(1)
    cont = fc_extension.shape[0]
    inner, outer = fourier_matrix(points, cont)
    links = connectivity.T

    def stay(x):
        return pltpu.with_memory_space_constraint(jnp.asarray(x), pltpu.HBM)

    def like(x):
        return jax.ShapeDtypeStruct(x.shape, x.dtype)

    box = jax.ShapeDtypeStruct((2, 16, points), F32)
    pair = jax.ShapeDtypeStruct((2 * points, 2 * points), BF16)
    square = pltpu.VMEM((points, points), F32)
    parts = pltpu.VMEM((components, 2 * points, 2 * points), BF16)
    grid = pltpu.VMEM(fields.shape, F32)

    (b0, b1, b2, b3, own, card, rate, left, right, fields, density, moduli, diag, cross) = pl.pallas_call(
        functools.partial(front_kernel, total=total),
        out_shape=[box] * 4
        + [
            jax.ShapeDtypeStruct((sides, 16, points), F32),
            jax.ShapeDtypeStruct((total, points), F32),
            like(fields),
            pair,
            pair,
        ]
        + [like(x) for x in (fields, density, moduli, diag, cross)],
        in_specs=[ANY] * 8 + [SMEM] * 3,
        out_specs=[VMEM] * 14,
        scratch_shapes=[
            square,
            pltpu.VMEM((points, cont), F32),
            pltpu.VMEM((fc_extension.shape[1], cont), F32),
            square,
            parts,
            parts,
            grid,
            grid,
            pltpu.SemaphoreType.DMA((7 + components,)),
        ],
        compiler_params=PARAMS,
        name="front",
    )(*[stay(x) for x in (fields, density, moduli, diag, cross, inner, outer, fc_extension.T)], links, patch_count, me)
    cards = lax.all_to_all(card, PATCH_SUB, 0, 0, tiled=True)
    arrived = [
        lax.ppermute(b, PATCH_SUB, [(i, (i + offset) % total) for i in range(total)])
        for b, offset in zip((b0, b1, b2, b3), offsets(total))
    ]
    line = pltpu.VMEM((sides, 8, points), F32)
    return pl.pallas_call(
        functools.partial(last_kernel, total=total, scale=scale),
        out_shape=like(fields),
        in_specs=[VMEM] * 14 + [SMEM] * 3,
        out_specs=ANY,
        scratch_shapes=[
            pltpu.VMEM((2 * sides, 16, points), F32),
            line,
            line,
            pltpu.VMEM((5, 2 * sides, points), F32),
            square,
            square,
            square,
            parts,
            parts,
            grid,
            grid,
            grid,
            grid,
            pltpu.SemaphoreType.DMA((components * slots,)),
        ],
        compiler_params=PARAMS,
        name="last",
    )(fields, rate, density, moduli, diag, cross, left, right, own, cards, *arrived, links, patch_count, me)


def solution(mesh):
    torus = Mesh(
        mesh.devices.reshape(4, 8, 4, mesh.shape["sub"]), ("patch_0", "patch_1", "patch_2", "sub")
    )
    return jax.shard_map(
        shards,
        mesh=torus,
        in_specs=(
            P(None, PATCH_SUB, None, None),
            P(PATCH_SUB, None, None),
            P(None, PATCH_SUB, None, None),
            P(None, PATCH_SUB, None, None),
            P(None, PATCH_SUB, None, None),
            P(),
            P(PATCH_SUB),
            P(PATCH_SUB, None),
        ),
        out_specs=P(None, PATCH_SUB, None, None),
        check_vma=False,
    )
```

time: 165 us -> 42.9 us (0.26)
  the two profiles are of different devices: /device:TPU:8 before, /device:TPU:103 now
where the time goes in v2:
time: 42.9 us; the launch traced here: 42.8 us
  starting transfers between devices  24.8 us (58%)
  waiting for transfers between devices  8.88 us (21%)
  Pallas kernels  7.68 us (18%)
  between operations  0.69 us (2%)
  local copies, waits for them, and re-layouts  0.67 us (2%)
    all_to_all x1, starting transfers between devices, shards(): cards = lax.all_to_all(card, PATCH_SUB, 0, 0, tiled=True)  14.3 us
    ppermute x4, starting transfers between devices, shards(): lax.ppermute(b, PATCH_SUB, [(i, (i + offset) % total) for i in range(tota...  10.6 us
    ppermute x4, waiting for transfers between devices, shards(): lax.ppermute(b, PATCH_SUB, [(i, (i + offset) % total) for i in range(tota...  8.88 us
    pallas_call x1, Pallas kernels, shards(): pl.pallas_call(functools.partial(front_kernel, total=total), out_shape=[b...  4.73 us
    pallas_call x1, Pallas kernels, shards(): pl.pallas_call(functools.partial(last_kernel, total=total, scale=scale),...  2.95 us
  transfers between devices with their start and end apart: 5, of which 2 were waited for; matrix products, arithmetic and copies ran while one was open for 0% of the time, Pallas kernels for 0%

profile of v2, /device:TPU:103, one launch (start us, length us, event | category | flops | bytes accessed | tf_op | source)
XLA Modules:
  0.0 42.8 jit_solution(15932187404200372684)
XLA Ops:
  0.7 0.0 copy-start
  0.7 0.7 %copy-done = s32[8,3]{0,1:T(4,128)S(1)} copy-done((s32[8,3]{0,1:T(4,128)S(1)}, s32[8,3]{0,1:T(4,128)}, u32[]{:S(2)}) %copy-start) | copy-done | bytes 120
  1.3 4.7 %front.1 = (f32[2,16,128]{2,1,0:T(8,128)S(1)}, f32[2,16,128]{2,1,0:T(8,128)S(1)}, f32[2,16,128]{2,1,0:T(8,128)S(1)}, f32[2,16,128]{2,1,0:T(8,128)S(1)}, f32[8,16...) custom-call(f32[5,2,128,128]{3,2,1,0:T(8,128)} %fields_in.1, ...), custom_call_target="tpu_custom_call" | custom-call | tf_op jit(solution)/shard_map/front/pallas_call | solution.py:399
  6.1 14.3 %all-to-all-start = ((f32[256,1,128]{2,1,0:T(1,128)}), f32[256,1,128]{2,1,0:T(1,128)S(1)}, u32[]{:S(2)}, u32[]{:S(2)}) async-start(f32[256,1,128]{2,1,0:T(1,128)} %bitcast.4), calls=%async_computation | async-start | bytes 262144 | tf_op jit(solution)/shard_map/all_to_all | solution.py:426
  20.4 3.0 %collective-permute-start = (f32[2,16,128]{2,1,0:T(8,128)S(1)}, f32[2,16,128]{2,1,0:T(8,128)S(1)}, u32[]{:S(2)}, u32[]{:S(2)}) collective-permute-start(f32[2,16,128]{2,1,0:T(8,128)S(1)} %get-tuple-element.29), channel_id=1, source_target_pairs={{0,1},{1,2},{2,3},{3,4},{4,5},{5,6},{6,7},{7,8},{8,9},{9,10},{10,1... | collective-permute-start | bytes 49160 | tf_op jit(solution)/shard_map/ppermute | solution.py:428
  23.3 0.0 collective-permute-start.1
  23.3 7.6 %collective-permute-start.2 = (f32[2,16,128]{2,1,0:T(8,128)S(1)}, f32[2,16,128]{2,1,0:T(8,128)S(1)}, u32[]{:S(2)}, u32[]{:S(2)}) collective-permute-start(f32[2,16,128]{2,1,0:T(8,128)S(1)} %get-tuple-element.31), channel_id=1, source_target_pairs={{0,129},{1,130},{2,131},{3,132},{4,133},{5,134},{6,135},{7,136},{8... | collective-permute-start | bytes 49160 | tf_op jit(solution)/shard_map/ppermute | solution.py:428
  30.9 0.0 collective-permute-start.3
  30.9 0.0 collective-permute-done.in0
  30.9 0.0 collective-permute-done.1.in1
  30.9 0.9 %collective-permute-done.2.in2 = f32[2,16,128]{2,1,0:T(8,128)S(1)} collective-permute-done((f32[2,16,128]{2,1,0:T(8,128)S(1)}, f32[2,16,128]{2,1,0:T(8,128)S(1)}, u32[]{:S(2)}, u32[]{:S(2)}) %collective-permute-start.2) | collective-permute-done | bytes 16416 | tf_op jit(solution)/shard_map/ppermute | solution.py:428
  31.8 8.0 %collective-permute-done.3.in3 = f32[2,16,128]{2,1,0:T(8,128)S(1)} collective-permute-done((f32[2,16,128]{2,1,0:T(8,128)S(1)}, f32[2,16,128]{2,1,0:T(8,128)S(1)}, u32[]{:S(2)}, u32[]{:S(2)}) %collective-permute-start.3) | collective-permute-done | bytes 16416 | tf_op jit(solution)/shard_map/ppermute | solution.py:428
  39.8 0.0 all-to-all-done
  39.8 3.0 %last.1 = f32[5,2,128,128]{3,2,1,0:T(8,128)} custom-call(f32[5,2,128,128]{3,2,1,0:T(8,128)S(1)} %get-tuple-element.19.fields_ref, f32[5,2,128,128]{3,2,1,0:T(8,128)S(1)} %get-tuple-element.20.inside_ref, f32[2,128,128]{2,1,0:T(8,128)S(1)} %get-tuple-element.21.density_ref, f32[2,2,128,128]{3,2,1,0:T(8,128)S(1)} %get-tuple-element.22.moduli_ref, ...), custom_call_target="tpu_custom_call" | custom-call | tf_op jit(solution)/shard_map/last/pallas_call | solution.py:432
Async XLA Ops:
  0.7 0.7 %copy-start = (s32[8,3]{0,1:T(4,128)S(1)}, s32[8,3]{0,1:T(4,128)}, u32[]{:S(2)}) copy-start(s32[8,3]{0,1:T(4,128)} %param.17) | copy-start | bytes 292
  6.1 33.7 %all-to-all-start = ((f32[256,1,128]{2,1,0:T(1,128)}), f32[256,1,128]{2,1,0:T(1,128)S(1)}, u32[]{:S(2)}, u32[]{:S(2)}) async-start(f32[256,1,128]{2,1,0:T(1,128)} %bitcast.4), calls=%async_computation | async-start | bytes 262144 | tf_op jit(solution)/shard_map/all_to_all | solution.py:426
  20.4 10.6 %collective-permute-start = (f32[2,16,128]{2,1,0:T(8,128)S(1)}, f32[2,16,128]{2,1,0:T(8,128)S(1)}, u32[]{:S(2)}, u32[]{:S(2)}) collective-permute-start(f32[2,16,128]{2,1,0:T(8,128)S(1)} %get-tuple-element.29), channel_id=1, source_target_pairs={{0,1},{1,2},{2,3},{3,4},{4,5},{5,6},{6,7},{7,8},{8,9},{9,10},{10,1... | collective-permute-start | bytes 49160 | tf_op jit(solution)/shard_map/ppermute | solution.py:428
  23.3 7.6 %collective-permute-start.1 = (f32[2,16,128]{2,1,0:T(8,128)S(1)}, f32[2,16,128]{2,1,0:T(8,128)S(1)}, u32[]{:S(2)}, u32[]{:S(2)}) collective-permute-start(f32[2,16,128]{2,1,0:T(8,128)S(1)} %get-tuple-element.30), channel_id=1, source_target_pairs={{0,255},{1,0},{2,1},{3,2},{4,3},{5,4},{6,5},{7,6},{8,7},{9,8},{10,... | collective-permute-start | bytes 49160 | tf_op jit(solution)/shard_map/ppermute | solution.py:428
  23.3 8.5 %collective-permute-start.2 = (f32[2,16,128]{2,1,0:T(8,128)S(1)}, f32[2,16,128]{2,1,0:T(8,128)S(1)}, u32[]{:S(2)}, u32[]{:S(2)}) collective-permute-start(f32[2,16,128]{2,1,0:T(8,128)S(1)} %get-tuple-element.31), channel_id=1, source_target_pairs={{0,129},{1,130},{2,131},{3,132},{4,133},{5,134},{6,135},{7,136},{8... | collective-permute-start | bytes 49160 | tf_op jit(solution)/shard_map/ppermute | solution.py:428
  30.9 8.9 %collective-permute-start.3 = (f32[2,16,128]{2,1,0:T(8,128)S(1)}, f32[2,16,128]{2,1,0:T(8,128)S(1)}, u32[]{:S(2)}, u32[]{:S(2)}) collective-permute-start(f32[2,16,128]{2,1,0:T(8,128)S(1)} %get-tuple-element.32), channel_id=1, source_target_pairs={{0,127},{1,128},{2,129},{3,130},{4,131},{5,132},{6,133},{7,134},{8... | collective-permute-start | bytes 49160 | tf_op jit(solution)/shard_map/ppermute | solution.py:428

commit v3 on v2

--- a/solution.py
+++ b/solution.py
@@ -37,6 +37,21 @@
 def offsets(total):
     step = total // 2 + 1
     return (1, -1, step, -step)
+
+
+ORDER = (3, 1, 2, 0)
+
+
+def routes(total):
+    return [
+        [(i, (i + (offset if i % 2 == 0 else -offset)) % total) for i in range(total)]
+        for offset in (offsets(total)[k] for k in ORDER)
+    ]
+
+
+def partners(me, total):
+    sign = jnp.where(lax.rem(me, 2) == 0, 1, -1)
+    return [lax.rem(me + sign * offsets(total)[k] + total, total) for k in ORDER]
 
 
 def lane_ids(shape):
@@ -149,10 +164,10 @@
 
 
 def front_kernel(
-    fields_in, density_in, moduli_in, diag_in, cross_in, inner_in, outer_in, ext_in, conn_ref, count_ref, me_ref,
+    fields_in, density_in, moduli_in, diag_in, cross_in, inner_in, outer_in, ext_in, conn_in, count_ref,
     out0, out1, out2, out3, own_ref, card_ref, rate_ref, left_ref, right_ref,
-    fields_ref, density_ref, moduli_ref, diag_ref, cross_ref,
-    inner_ref, outer_ref, ext_ref, scr_ref, cols_ref, rows_ref, xi_ref, eta_ref, sems, *, total,
+    fields_ref, density_ref, moduli_ref, diag_ref, cross_ref, links_ref,
+    inner_ref, outer_ref, ext_ref, scr_ref, cols_ref, rows_ref, xi_ref, eta_ref, conn_ref, sems, *, total,
 ):
     fields, slots, points, _ = fields_ref.shape
     sides = 4 * slots
@@ -170,6 +185,7 @@
             ((density_in, density_ref), (moduli_in, moduli_ref), (diag_in, diag_ref), (cross_in, cross_ref))
         )
     ]
+    links = [fetch(conn_in, conn_ref, 7 + fields), fetch(conn_in, links_ref, 8 + fields)]
     for copy in small:
         copy.wait()
     build_matrices(inner_ref[...], outer_ref[...], ext_ref[...], left_ref, right_ref)
@@ -179,7 +195,7 @@
             f, lambda s, f=f: fields_ref[f, s], left_ref, right_ref, cols_ref, rows_ref, xi_ref, eta_ref, slots, points
         )
     boundary_lines(fields_ref, own_ref, 0, scr_ref, fields, slots, points)
-    for copy in coefs:
+    for copy in coefs + links:
         copy.wait()
 
     peak = jnp.zeros((8, points), F32)
@@ -220,8 +236,7 @@
             card = jnp.where(lane == CONN_LANE + 3 * i + c, conn_ref[c, i].astype(F32), card)
     card_ref[...] = jnp.broadcast_to(card, card_ref.shape)
 
-    for offset, out_ref in zip(offsets(total), (out0, out1, out2, out3)):
-        partner = lax.rem(me_ref[0] + offset + total, total)
+    for partner, out_ref in zip(partners(lax.axis_index(PATCH_SUB), total), (out0, out1, out2, out3)):
         first = jnp.int32(0)
         second = jnp.int32(0)
         count = jnp.int32(0)
@@ -288,7 +303,7 @@
 
 def last_kernel(
     fields_ref, inside_ref, density_ref, moduli_ref, diag_ref, cross_ref, left_ref, right_ref, own_ref, cards_ref,
-    in0, in1, in2, in3, conn_ref, count_ref, me_ref,
+    in0, in1, in2, in3, conn_ref, count_ref,
     final_out,
     table_ref, jump_ref, mine_ref, near_ref, scr_ref, turned_ref, corner_ref,
     cols_ref, rows_ref, xi_ref, eta_ref, rate_ref, final_ref, sems, *, total, scale,
@@ -314,9 +329,8 @@
                 before = (conn_ref[0, j] == owner) & (conn_ref[1, j] < strip)
                 position = position + before.astype(jnp.int32)
         place = strip
-        for k, offset in enumerate(offsets(total)):
-            source = lax.rem(me_ref[0] - offset + total, total)
-            place = jnp.where(owner == source, sides + 2 * k + position, place)
+        for k, partner in enumerate(partners(lax.axis_index(PATCH_SUB), total)):
+            place = jnp.where(owner == partner, sides + 2 * k + position, place)
         place = jnp.clip(place, 0, 2 * sides - 1)
         index = jnp.where(conn_ref[2, i] == 1, points - 1 - lanes, lanes)
         line = jnp.take_along_axis(table_ref[place, pl.ds(0, 8), :], index, axis=1)
@@ -379,7 +393,6 @@
     total = lax.axis_size(PATCH_SUB)
     scale = PENALTY * (points - 1)
     sides = 4 * slots
-    me = lax.axis_index(PATCH_SUB).reshape(1)
     cont = fc_extension.shape[0]
     inner, outer = fourier_matrix(points, cont)
     links = connectivity.T
@@ -396,7 +409,7 @@
     parts = pltpu.VMEM((components, 2 * points, 2 * points), BF16)
     grid = pltpu.VMEM(fields.shape, F32)
 
-    (b0, b1, b2, b3, own, card, rate, left, right, fields, density, moduli, diag, cross) = pl.pallas_call(
+    (b0, b1, b2, b3, own, card, rate, left, right, fields, density, moduli, diag, cross, held) = pl.pallas_call(
         functools.partial(front_kernel, total=total),
         out_shape=[box] * 4
         + [
@@ -406,9 +419,9 @@
             pair,
             pair,
         ]
-        + [like(x) for x in (fields, density, moduli, diag, cross)],
-        in_specs=[ANY] * 8 + [SMEM] * 3,
-        out_specs=[VMEM] * 14,
+        + [like(x) for x in (fields, density, moduli, diag, cross, links)],
+        in_specs=[ANY] * 9 + [SMEM],
+        out_specs=[VMEM] * 15,
         scratch_shapes=[
             square,
             pltpu.VMEM((points, cont), F32),
@@ -418,21 +431,19 @@
             parts,
             grid,
             grid,
-            pltpu.SemaphoreType.DMA((7 + components,)),
+            pltpu.SMEM(links.shape, jnp.int32),
+            pltpu.SemaphoreType.DMA((9 + components,)),
         ],
         compiler_params=PARAMS,
         name="front",
-    )(*[stay(x) for x in (fields, density, moduli, diag, cross, inner, outer, fc_extension.T)], links, patch_count, me)
+    )(*[stay(x) for x in (fields, density, moduli, diag, cross, inner, outer, fc_extension.T, links)], patch_count)
     cards = lax.all_to_all(card, PATCH_SUB, 0, 0, tiled=True)
-    arrived = [
-        lax.ppermute(b, PATCH_SUB, [(i, (i + offset) % total) for i in range(total)])
-        for b, offset in zip((b0, b1, b2, b3), offsets(total))
-    ]
+    arrived = [lax.ppermute(b, PATCH_SUB, route) for b, route in zip((b0, b1, b2, b3), routes(total))]
     line = pltpu.VMEM((sides, 8, points), F32)
     return pl.pallas_call(
         functools.partial(last_kernel, total=total, scale=scale),
         out_shape=like(fields),
-        in_specs=[VMEM] * 14 + [SMEM] * 3,
+        in_specs=[VMEM] * 14 + [SMEM] * 2,
         out_specs=ANY,
         scratch_shapes=[
             pltpu.VMEM((2 * sides, 16, points), F32),
@@ -452,7 +463,7 @@
         ],
         compiler_params=PARAMS,
         name="last",
-    )(fields, rate, density, moduli, diag, cross, left, right, own, cards, *arrived, links, patch_count, me)
+    )(fields, rate, density, moduli, diag, cross, left, right, own, cards, *arrived, held, patch_count)
 
 
 def solution(mesh):

time: 42.9 us -> 37.4 us (0.87)
  the two profiles are of different devices: /device:TPU:103 before, /device:TPU:8 now
where the time goes in v3:
time: 37.4 us; the launch traced here: 37.3 us
  starting transfers between devices  23.7 us (63%)
  Pallas kernels  7.17 us (19%)
  waiting for transfers between devices  5.71 us (15%)
  between operations  0.68 us (2%)
    all_to_all x1, starting transfers between devices, shards(): cards = lax.all_to_all(card, PATCH_SUB, 0, 0, tiled=True)  14.6 us
    ppermute x4, starting transfers between devices, shards(): lax.ppermute(b, PATCH_SUB, route)  9.09 us
    ppermute x4, waiting for transfers between devices, shards(): lax.ppermute(b, PATCH_SUB, route)  5.71 us
    pallas_call x1, Pallas kernels, shards(): pl.pallas_call(functools.partial(front_kernel, total=total), out_shape=[b...  4.2 us
    pallas_call x1, Pallas kernels, shards(): pl.pallas_call(functools.partial(last_kernel, total=total, scale=scale),...  2.97 us
  transfers between devices with their start and end apart: 5, of which 2 were waited for; matrix products, arithmetic and copies ran while one was open for 0% of the time, Pallas kernels for 0%

profile of v3, /device:TPU:8, one launch (start us, length us, event | category | flops | bytes accessed | tf_op | source)
XLA Modules:
  0.0 37.3 jit_solution(15644222977976219101)
XLA Ops:
  0.7 4.2 %front.1 = (f32[2,16,128]{2,1,0:T(8,128)S(1)}, f32[2,16,128]{2,1,0:T(8,128)S(1)}, f32[2,16,128]{2,1,0:T(8,128)S(1)}, f32[2,16,128]{2,1,0:T(8,128)S(1)}, f32[8,16...) custom-call(f32[5,2,128,128]{3,2,1,0:T(8,128)} %fields_in.1, ...), custom_call_target="tpu_custom_call" | custom-call | tf_op jit(solution)/shard_map/front/pallas_call | solution.py:412
  4.9 14.6 %all-to-all-start = ((f32[256,1,128]{2,1,0:T(1,128)}), f32[256,1,128]{2,1,0:T(1,128)S(1)}, u32[]{:S(2)}, u32[]{:S(2)}) async-start(f32[256,1,128]{2,1,0:T(1,128)} %bitcast.3), calls=%async_computation | async-start | bytes 262144 | tf_op jit(solution)/shard_map/all_to_all | solution.py:440
  19.5 7.4 %collective-permute-start = (f32[2,16,128]{2,1,0:T(8,128)S(1)}, f32[2,16,128]{2,1,0:T(8,128)S(1)}, u32[]{:S(2)}, u32[]{:S(2)}) collective-permute-start(f32[2,16,128]{2,1,0:T(8,128)S(1)} %get-tuple-element.30), channel_id=1, source_target_pairs={{0,127},{1,130},{2,129},{3,132},{4,131},{5,134},{6,133},{7,136},{8... | collective-permute-start | bytes 49160 | tf_op jit(solution)/shard_map/ppermute | solution.py:441
  26.9 0.0 collective-permute-start.1
  26.9 0.0 collective-permute-start.2
  26.9 1.7 %collective-permute-start.3 = (f32[2,16,128]{2,1,0:T(8,128)S(1)}, f32[2,16,128]{2,1,0:T(8,128)S(1)}, u32[]{:S(2)}, u32[]{:S(2)}) collective-permute-start(f32[2,16,128]{2,1,0:T(8,128)S(1)} %get-tuple-element.33), channel_id=1, source_target_pairs={{0,1},{1,0},{2,3},{3,2},{4,5},{5,4},{6,7},{7,6},{8,9},{9,8},{10,11... | collective-permute-start | bytes 49160 | tf_op jit(solution)/shard_map/ppermute | solution.py:441
  28.6 0.8 %collective-permute-done.in0 = f32[2,16,128]{2,1,0:T(8,128)S(1)} collective-permute-done((f32[2,16,128]{2,1,0:T(8,128)S(1)}, f32[2,16,128]{2,1,0:T(8,128)S(1)}, u32[]{:S(2)}, u32[]{:S(2)}) %collective-permute-start) | collective-permute-done | bytes 16416 | tf_op jit(solution)/shard_map/ppermute | solution.py:441
  29.4 4.9 %collective-permute-done.1.in1 = f32[2,16,128]{2,1,0:T(8,128)S(1)} collective-permute-done((f32[2,16,128]{2,1,0:T(8,128)S(1)}, f32[2,16,128]{2,1,0:T(8,128)S(1)}, u32[]{:S(2)}, u32[]{:S(2)}) %collective-permute-start.1) | collective-permute-done | bytes 16416 | tf_op jit(solution)/shard_map/ppermute | solution.py:441
  34.3 0.0 collective-permute-done.2.in2
  34.3 0.0 collective-permute-done.3.in3
  34.3 0.0 all-to-all-done
  34.3 3.0 %last.1 = f32[5,2,128,128]{3,2,1,0:T(8,128)} custom-call(f32[5,2,128,128]{3,2,1,0:T(8,128)S(1)} %get-tuple-element.20.fields_ref, f32[5,2,128,128]{3,2,1,0:T(8,128)S(1)} %get-tuple-element.21.inside_ref, f32[2,128,128]{2,1,0:T(8,128)S(1)} %get-tuple-element.22.density_ref, f32[2,2,128,128]{3,2,1,0:T(8,128)S(1)} %get-tuple-element.23.moduli_ref, ...), custom_call_target="tpu_custom_call" | custom-call | tf_op jit(solution)/shard_map/last/pallas_call | solution.py:443
Async XLA Ops:
  4.9 29.4 %all-to-all-start = ((f32[256,1,128]{2,1,0:T(1,128)}), f32[256,1,128]{2,1,0:T(1,128)S(1)}, u32[]{:S(2)}, u32[]{:S(2)}) async-start(f32[256,1,128]{2,1,0:T(1,128)} %bitcast.3), calls=%async_computation | async-start | bytes 262144 | tf_op jit(solution)/shard_map/all_to_all | solution.py:440
  19.5 9.9 %collective-permute-start = (f32[2,16,128]{2,1,0:T(8,128)S(1)}, f32[2,16,128]{2,1,0:T(8,128)S(1)}, u32[]{:S(2)}, u32[]{:S(2)}) collective-permute-start(f32[2,16,128]{2,1,0:T(8,128)S(1)} %get-tuple-element.30), channel_id=1, source_target_pairs={{0,127},{1,130},{2,129},{3,132},{4,131},{5,134},{6,133},{7,136},{8... | collective-permute-start | bytes 49160 | tf_op jit(solution)/shard_map/ppermute | solution.py:441
  26.9 7.4 %collective-permute-start.1 = (f32[2,16,128]{2,1,0:T(8,128)S(1)}, f32[2,16,128]{2,1,0:T(8,128)S(1)}, u32[]{:S(2)}, u32[]{:S(2)}) collective-permute-start(f32[2,16,128]{2,1,0:T(8,128)S(1)} %get-tuple-element.31), channel_id=1, source_target_pairs={{0,255},{1,2},{2,1},{3,4},{4,3},{5,6},{6,5},{7,8},{8,7},{9,10},{10... | collective-permute-start | bytes 49160 | tf_op jit(solution)/shard_map/ppermute | solution.py:441
  26.9 7.4 %collective-permute-start.2 = (f32[2,16,128]{2,1,0:T(8,128)S(1)}, f32[2,16,128]{2,1,0:T(8,128)S(1)}, u32[]{:S(2)}, u32[]{:S(2)}) collective-permute-start(f32[2,16,128]{2,1,0:T(8,128)S(1)} %get-tuple-element.32), channel_id=1, source_target_pairs={{0,129},{1,128},{2,131},{3,130},{4,133},{5,132},{6,135},{7,134},{8... | collective-permute-start | bytes 49160 | tf_op jit(solution)/shard_map/ppermute | solution.py:441
  26.9 7.4 %collective-permute-start.3 = (f32[2,16,128]{2,1,0:T(8,128)S(1)}, f32[2,16,128]{2,1,0:T(8,128)S(1)}, u32[]{:S(2)}, u32[]{:S(2)}) collective-permute-start(f32[2,16,128]{2,1,0:T(8,128)S(1)} %get-tuple-element.33), channel_id=1, source_target_pairs={{0,1},{1,0},{2,3},{3,2},{4,5},{5,4},{6,7},{7,6},{8,9},{9,8},{10,11... | collective-permute-start | bytes 49160 | tf_op jit(solution)/shard_map/ppermute | solution.py:441

commit v4 on v3

--- a/solution.py
+++ b/solution.py
@@ -139,16 +139,12 @@
     )
 
 
-def build_matrices(inner, outer, ext, left_ref, right_ref):
+def build_matrices(inner, outer, ext, match, left_ref, right_ref):
     points = inner.shape[0]
-    match = ext.shape[0] // 2
-    rows = lax.broadcasted_iota(jnp.int32, (2 * match, points), 0)
-    lanes = lane_ids((2 * match, points))
-    place = jnp.where(rows < match, points - match + rows, rows - match)
-    spread = jnp.where(lanes == place, 1.0, 0.0).astype(F32)
-    exact = dict(precision=lax.Precision.HIGHEST, preferred_element_type=F32)
-    wide = lax.dot_general(ext, spread, (((0,), (0,)), ((), ())), **exact)
-    full = inner + jnp.dot(outer, wide, **exact)
+    folded = lax.dot_general(
+        outer, ext, (((1,), (1,)), ((), ())), precision=lax.Precision.HIGHEST, preferred_element_type=F32
+    )
+    full = inner + pltpu.roll(folded, points - match, 1)
     zero = jnp.zeros((points, points), BF16)
     first, second = pl.ds(0, points), pl.ds(points, points)
     high, low = split(full)
@@ -167,34 +163,30 @@
     fields_in, density_in, moduli_in, diag_in, cross_in, inner_in, outer_in, ext_in, conn_in, count_ref,
     out0, out1, out2, out3, own_ref, card_ref, rate_ref, left_ref, right_ref,
     fields_ref, density_ref, moduli_ref, diag_ref, cross_ref, links_ref,
-    inner_ref, outer_ref, ext_ref, scr_ref, cols_ref, rows_ref, xi_ref, eta_ref, conn_ref, sems, *, total,
+    inner_ref, outer_ref, ext_ref, scr_ref, cols_ref, rows_ref, xi_ref, eta_ref, conn_ref, rows_out_ref, sems, *, total,
 ):
     fields, slots, points, _ = fields_ref.shape
     sides = 4 * slots
+
+    ext_ref[...] = jnp.zeros(ext_ref.shape, F32)
 
     def fetch(source, target, at):
         copy = pltpu.make_async_copy(source, target, sems.at[at])
         copy.start()
         return copy
 
-    small = [fetch(a, b, i) for i, (a, b) in enumerate(((inner_in, inner_ref), (outer_in, outer_ref), (ext_in, ext_ref)))]
-    large = [fetch(fields_in.at[f], fields_ref.at[f], 3 + f) for f in range(fields)]
+    small = [fetch(a, b, i) for i, (a, b) in enumerate(((inner_in, inner_ref), (outer_in, outer_ref), (ext_in, ext_ref.at[pl.ds(0, ext_in.shape[0])])))]
     coefs = [
         fetch(a, b, 3 + fields + i)
         for i, (a, b) in enumerate(
             ((density_in, density_ref), (moduli_in, moduli_ref), (diag_in, diag_ref), (cross_in, cross_ref))
         )
     ]
+    large = [fetch(fields_in.at[f], fields_ref.at[f], 3 + f) for f in range(fields)]
     links = [fetch(conn_in, conn_ref, 7 + fields), fetch(conn_in, links_ref, 8 + fields)]
     for copy in small:
         copy.wait()
-    build_matrices(inner_ref[...], outer_ref[...], ext_ref[...], left_ref, right_ref)
-    for f in range(fields):
-        large[f].wait()
-        derivatives(
-            f, lambda s, f=f: fields_ref[f, s], left_ref, right_ref, cols_ref, rows_ref, xi_ref, eta_ref, slots, points
-        )
-    boundary_lines(fields_ref, own_ref, 0, scr_ref, fields, slots, points)
+    build_matrices(inner_ref[...], outer_ref[...], ext_ref[...], ext_in.shape[0] // 2, left_ref, right_ref)
     for copy in coefs + links:
         copy.wait()
 
@@ -212,12 +204,11 @@
             speed = jnp.where(live, speed, 0.0)
             for r in range(CHUNK // 8):
                 peak = jnp.maximum(peak, speed[8 * r : 8 * r + 8])
-            parts = assemble(s, rows, density_ref, moduli_ref, diag_ref, cross_ref, xi_ref, eta_ref)
-            for f in range(fields):
-                rate_ref[f, s, rows, :] = parts[f]
     peak = jnp.max(jnp.max(peak, axis=0, keepdims=True), axis=1, keepdims=True)
-    boundary_lines(rate_ref, own_ref, 8, scr_ref, fields, slots, points)
-
+
+    for copy in large:
+        copy.wait()
+    boundary_lines(fields_ref, own_ref, 0, scr_ref, fields, slots, points)
     lanes = lane_ids((8, points))
     corners = jnp.zeros((8, points), F32)
     for s in range(slots):
@@ -234,7 +225,20 @@
     for i in range(sides):
         for c in range(3):
             card = jnp.where(lane == CONN_LANE + 3 * i + c, conn_ref[c, i].astype(F32), card)
-    card_ref[...] = jnp.broadcast_to(card, card_ref.shape)
+    rows_out_ref[...] = jnp.broadcast_to(card, rows_out_ref.shape)
+    sent = fetch(rows_out_ref, card_ref, 9 + fields)
+
+    for f in range(fields):
+        derivatives(
+            f, lambda s, f=f: fields_ref[f, s], left_ref, right_ref, cols_ref, rows_ref, xi_ref, eta_ref, slots, points
+        )
+    for s in range(slots):
+        for c in range(points // CHUNK):
+            rows = pl.ds(c * CHUNK, CHUNK)
+            parts = assemble(s, rows, density_ref, moduli_ref, diag_ref, cross_ref, xi_ref, eta_ref)
+            for f in range(fields):
+                rate_ref[f, s, rows, :] = parts[f]
+    boundary_lines(rate_ref, own_ref, 8, scr_ref, fields, slots, points)
 
     for partner, out_ref in zip(partners(lax.axis_index(PATCH_SUB), total), (out0, out1, out2, out3)):
         first = jnp.int32(0)
@@ -247,6 +251,7 @@
             count = count + match.astype(jnp.int32)
         out_ref[0] = own_ref[first]
         out_ref[1] = own_ref[second]
+    sent.wait()
 
 
 def corner_terms(cards_ref, conn_ref, near_ref, total, sides, points):
@@ -421,18 +426,19 @@
         ]
         + [like(x) for x in (fields, density, moduli, diag, cross, links)],
         in_specs=[ANY] * 9 + [SMEM],
-        out_specs=[VMEM] * 15,
+        out_specs=[VMEM] * 5 + [ANY] + [VMEM] * 9,
         scratch_shapes=[
             square,
             pltpu.VMEM((points, cont), F32),
-            pltpu.VMEM((fc_extension.shape[1], cont), F32),
+            pltpu.VMEM((points, cont), F32),
             square,
             parts,
             parts,
             grid,
             grid,
             pltpu.SMEM(links.shape, jnp.int32),
-            pltpu.SemaphoreType.DMA((9 + components,)),
+            pltpu.VMEM((total, points), F32),
+            pltpu.SemaphoreType.DMA((10 + components,)),
         ],
         compiler_params=PARAMS,
         name="front",

time: 37.4 us -> 36.4 us (0.973)
  Pallas kernels: 7.17 us -> 6.15 us
    pallas_call x1, Pallas kernels: 4.2 us -> 3.18 us  [shards(): pl.pallas_call(functools.partial(front_kernel, total=total), out_shape=[b...]
where the time goes in v4:
time: 36.4 us; the launch traced here: 36.2 us
  starting transfers between devices  23.7 us (65%)
  Pallas kernels  6.15 us (17%)
  waiting for transfers between devices  5.71 us (16%)
  between operations  0.68 us (2%)
    all_to_all x1, starting transfers between devices, shards(): cards = lax.all_to_all(card, PATCH_SUB, 0, 0, tiled=True)  14.6 us
    ppermute x4, starting transfers between devices, shards(): lax.ppermute(b, PATCH_SUB, route)  9.09 us
    ppermute x4, waiting for transfers between devices, shards(): lax.ppermute(b, PATCH_SUB, route)  5.71 us
    pallas_call x1, Pallas kernels, shards(): pl.pallas_call(functools.partial(front_kernel, total=total), out_shape=[b...  3.18 us
    pallas_call x1, Pallas kernels, shards(): pl.pallas_call(functools.partial(last_kernel, total=total, scale=scale),...  2.97 us
  transfers between devices with their start and end apart: 5, of which 2 were waited for; matrix products, arithmetic and copies ran while one was open for 0% of the time, Pallas kernels for 0%

profile of v4, /device:TPU:8, one launch (start us, length us, event | category | flops | bytes accessed | tf_op | source)
XLA Modules:
  0.0 36.2 jit_solution(13792052564382420478)
XLA Ops:
  0.7 3.2 %front.1 = (f32[2,16,128]{2,1,0:T(8,128)S(1)}, f32[2,16,128]{2,1,0:T(8,128)S(1)}, f32[2,16,128]{2,1,0:T(8,128)S(1)}, f32[2,16,128]{2,1,0:T(8,128)S(1)}, f32[8,16...) custom-call(f32[5,2,128,128]{3,2,1,0:T(8,128)} %fields_in.1, ...), custom_call_target="tpu_custom_call" | custom-call | tf_op jit(solution)/shard_map/front/pallas_call | solution.py:417
  3.8 14.6 %all-to-all-start = ((f32[256,1,128]{2,1,0:T(1,128)}), f32[256,1,128]{2,1,0:T(1,128)S(1)}, u32[]{:S(2)}, u32[]{:S(2)}) async-start(f32[256,1,128]{2,1,0:T(1,128)} %bitcast.3), calls=%async_computation | async-start | bytes 262144 | tf_op jit(solution)/shard_map/all_to_all | solution.py:446
  18.5 7.4 %collective-permute-start = (f32[2,16,128]{2,1,0:T(8,128)S(1)}, f32[2,16,128]{2,1,0:T(8,128)S(1)}, u32[]{:S(2)}, u32[]{:S(2)}) collective-permute-start(f32[2,16,128]{2,1,0:T(8,128)S(1)} %get-tuple-element.30), channel_id=1, source_target_pairs={{0,127},{1,130},{2,129},{3,132},{4,131},{5,134},{6,133},{7,136},{8... | collective-permute-start | bytes 49160 | tf_op jit(solution)/shard_map/ppermute | solution.py:447
  25.9 0.0 collective-permute-start.1
  25.9 0.0 collective-permute-start.2
  25.9 1.7 %collective-permute-start.3 = (f32[2,16,128]{2,1,0:T(8,128)S(1)}, f32[2,16,128]{2,1,0:T(8,128)S(1)}, u32[]{:S(2)}, u32[]{:S(2)}) collective-permute-start(f32[2,16,128]{2,1,0:T(8,128)S(1)} %get-tuple-element.33), channel_id=1, source_target_pairs={{0,1},{1,0},{2,3},{3,2},{4,5},{5,4},{6,7},{7,6},{8,9},{9,8},{10,11... | collective-permute-start | bytes 49160 | tf_op jit(solution)/shard_map/ppermute | solution.py:447
  27.6 0.8 %collective-permute-done.in0 = f32[2,16,128]{2,1,0:T(8,128)S(1)} collective-permute-done((f32[2,16,128]{2,1,0:T(8,128)S(1)}, f32[2,16,128]{2,1,0:T(8,128)S(1)}, u32[]{:S(2)}, u32[]{:S(2)}) %collective-permute-start) | collective-permute-done | bytes 16416 | tf_op jit(solution)/shard_map/ppermute | solution.py:447
  28.3 4.9 %collective-permute-done.1.in1 = f32[2,16,128]{2,1,0:T(8,128)S(1)} collective-permute-done((f32[2,16,128]{2,1,0:T(8,128)S(1)}, f32[2,16,128]{2,1,0:T(8,128)S(1)}, u32[]{:S(2)}, u32[]{:S(2)}) %collective-permute-start.1) | collective-permute-done | bytes 16416 | tf_op jit(solution)/shard_map/ppermute | solution.py:447
  33.3 0.0 collective-permute-done.2.in2
  33.3 0.0 collective-permute-done.3.in3
  33.3 0.0 all-to-all-done
  33.3 3.0 %last.1 = f32[5,2,128,128]{3,2,1,0:T(8,128)} custom-call(f32[5,2,128,128]{3,2,1,0:T(8,128)S(1)} %get-tuple-element.20.fields_ref, f32[5,2,128,128]{3,2,1,0:T(8,128)S(1)} %get-tuple-element.21.inside_ref, f32[2,128,128]{2,1,0:T(8,128)S(1)} %get-tuple-element.22.density_ref, f32[2,2,128,128]{3,2,1,0:T(8,128)S(1)} %get-tuple-element.23.moduli_ref, ...), custom_call_target="tpu_custom_call" | custom-call | tf_op jit(solution)/shard_map/last/pallas_call | solution.py:449
Async XLA Ops:
  3.8 29.4 %all-to-all-start = ((f32[256,1,128]{2,1,0:T(1,128)}), f32[256,1,128]{2,1,0:T(1,128)S(1)}, u32[]{:S(2)}, u32[]{:S(2)}) async-start(f32[256,1,128]{2,1,0:T(1,128)} %bitcast.3), calls=%async_computation | async-start | bytes 262144 | tf_op jit(solution)/shard_map/all_to_all | solution.py:446
  18.5 9.9 %collective-permute-start = (f32[2,16,128]{2,1,0:T(8,128)S(1)}, f32[2,16,128]{2,1,0:T(8,128)S(1)}, u32[]{:S(2)}, u32[]{:S(2)}) collective-permute-start(f32[2,16,128]{2,1,0:T(8,128)S(1)} %get-tuple-element.30), channel_id=1, source_target_pairs={{0,127},{1,130},{2,129},{3,132},{4,131},{5,134},{6,133},{7,136},{8... | collective-permute-start | bytes 49160 | tf_op jit(solution)/shard_map/ppermute | solution.py:447
  25.9 7.4 %collective-permute-start.1 = (f32[2,16,128]{2,1,0:T(8,128)S(1)}, f32[2,16,128]{2,1,0:T(8,128)S(1)}, u32[]{:S(2)}, u32[]{:S(2)}) collective-permute-start(f32[2,16,128]{2,1,0:T(8,128)S(1)} %get-tuple-element.31), channel_id=1, source_target_pairs={{0,255},{1,2},{2,1},{3,4},{4,3},{5,6},{6,5},{7,8},{8,7},{9,10},{10... | collective-permute-start | bytes 49160 | tf_op jit(solution)/shard_map/ppermute | solution.py:447
  25.9 7.4 %collective-permute-start.2 = (f32[2,16,128]{2,1,0:T(8,128)S(1)}, f32[2,16,128]{2,1,0:T(8,128)S(1)}, u32[]{:S(2)}, u32[]{:S(2)}) collective-permute-start(f32[2,16,128]{2,1,0:T(8,128)S(1)} %get-tuple-element.32), channel_id=1, source_target_pairs={{0,129},{1,128},{2,131},{3,130},{4,133},{5,132},{6,135},{7,134},{8... | collective-permute-start | bytes 49160 | tf_op jit(solution)/shard_map/ppermute | solution.py:447
  25.9 7.4 %collective-permute-start.3 = (f32[2,16,128]{2,1,0:T(8,128)S(1)}, f32[2,16,128]{2,1,0:T(8,128)S(1)}, u32[]{:S(2)}, u32[]{:S(2)}) collective-permute-start(f32[2,16,128]{2,1,0:T(8,128)S(1)} %get-tuple-element.33), channel_id=1, source_target_pairs={{0,1},{1,0},{2,3},{3,2},{4,5},{5,4},{6,7},{7,6},{8,9},{9,8},{10,11... | collective-permute-start | bytes 49160 | tf_op jit(solution)/shard_map/ppermute | solution.py:447

commit v5 on v4

--- a/solution.py
+++ b/solution.py
@@ -318,6 +318,8 @@
     lanes = lane_ids((8, points))
     scr_ref[...] = jnp.zeros(scr_ref.shape, F32)
 
+    corner_ref[...] = jnp.zeros(corner_ref.shape, F32)
+    corner_ref[pl.ds(0, 2 * sides), :] = corner_terms(cards_ref, conn_ref, near_ref, total, sides, points)
     for i in range(sides):
         table_ref[i] = own_ref[i]
     for k, in_ref in enumerate((in0, in1, in2, in3)):
@@ -364,8 +366,6 @@
     dt = CFL / (bound * (points - 1))
     half = 0.5 * dt * dt
 
-    corner_ref[...] = jnp.zeros(corner_ref.shape, F32)
-    corner_ref[pl.ds(0, 2 * sides), :] = corner_terms(cards_ref, conn_ref, near_ref, total, sides, points)
     corners = corner_ref[...].T[:8]
     for i in range(sides):
         partner = partner_rates[i] + scale * column_part(corners, 2 * i, points)

time: 36.4 us -> 36.2 us (level)
  no operation moved by 1% of the time
where the time goes in v5:
time: 36.2 us; the launch traced here: 36.1 us
  starting transfers between devices  23.7 us (65%)
  Pallas kernels  6 us (17%)
  waiting for transfers between devices  5.71 us (16%)
  between operations  0.68 us (2%)
    all_to_all x1, starting transfers between devices, shards(): cards = lax.all_to_all(card, PATCH_SUB, 0, 0, tiled=True)  14.6 us
    ppermute x4, starting transfers between devices, shards(): lax.ppermute(b, PATCH_SUB, route)  9.09 us
    ppermute x4, waiting for transfers between devices, shards(): lax.ppermute(b, PATCH_SUB, route)  5.71 us
    pallas_call x1, Pallas kernels, shards(): pl.pallas_call(functools.partial(front_kernel, total=total), out_shape=[b...  3.18 us
    pallas_call x1, Pallas kernels, shards(): pl.pallas_call(functools.partial(last_kernel, total=total, scale=scale),...  2.82 us
  transfers between devices with their start and end apart: 5, of which 2 were waited for; matrix products, arithmetic and copies ran while one was open for 0% of the time, Pallas kernels for 0%

profile of v5, /device:TPU:8, one launch (start us, length us, event | category | flops | bytes accessed | tf_op | source)
XLA Modules:
  0.0 36.1 jit_solution(398319420665576068)
XLA Ops:
  0.7 3.2 %front.1 = (f32[2,16,128]{2,1,0:T(8,128)S(1)}, f32[2,16,128]{2,1,0:T(8,128)S(1)}, f32[2,16,128]{2,1,0:T(8,128)S(1)}, f32[2,16,128]{2,1,0:T(8,128)S(1)}, f32[8,16...) custom-call(f32[5,2,128,128]{3,2,1,0:T(8,128)} %fields_in.1, ...), custom_call_target="tpu_custom_call" | custom-call | tf_op jit(solution)/shard_map/front/pallas_call | solution.py:417
  3.8 14.6 %all-to-all-start = ((f32[256,1,128]{2,1,0:T(1,128)}), f32[256,1,128]{2,1,0:T(1,128)S(1)}, u32[]{:S(2)}, u32[]{:S(2)}) async-start(f32[256,1,128]{2,1,0:T(1,128)} %bitcast.3), calls=%async_computation | async-start | bytes 262144 | tf_op jit(solution)/shard_map/all_to_all | solution.py:446
  18.5 7.4 %collective-permute-start = (f32[2,16,128]{2,1,0:T(8,128)S(1)}, f32[2,16,128]{2,1,0:T(8,128)S(1)}, u32[]{:S(2)}, u32[]{:S(2)}) collective-permute-start(f32[2,16,128]{2,1,0:T(8,128)S(1)} %get-tuple-element.30), channel_id=1, source_target_pairs={{0,127},{1,130},{2,129},{3,132},{4,131},{5,134},{6,133},{7,136},{8... | collective-permute-start | bytes 49160 | tf_op jit(solution)/shard_map/ppermute | solution.py:447
  25.9 0.0 collective-permute-start.1
  25.9 0.0 collective-permute-start.2
  25.9 1.7 %collective-permute-start.3 = (f32[2,16,128]{2,1,0:T(8,128)S(1)}, f32[2,16,128]{2,1,0:T(8,128)S(1)}, u32[]{:S(2)}, u32[]{:S(2)}) collective-permute-start(f32[2,16,128]{2,1,0:T(8,128)S(1)} %get-tuple-element.33), channel_id=1, source_target_pairs={{0,1},{1,0},{2,3},{3,2},{4,5},{5,4},{6,7},{7,6},{8,9},{9,8},{10,11... | collective-permute-start | bytes 49160 | tf_op jit(solution)/shard_map/ppermute | solution.py:447
  27.6 0.8 %collective-permute-done.in0 = f32[2,16,128]{2,1,0:T(8,128)S(1)} collective-permute-done((f32[2,16,128]{2,1,0:T(8,128)S(1)}, f32[2,16,128]{2,1,0:T(8,128)S(1)}, u32[]{:S(2)}, u32[]{:S(2)}) %collective-permute-start) | collective-permute-done | bytes 16416 | tf_op jit(solution)/shard_map/ppermute | solution.py:447
  28.3 4.9 %collective-permute-done.1.in1 = f32[2,16,128]{2,1,0:T(8,128)S(1)} collective-permute-done((f32[2,16,128]{2,1,0:T(8,128)S(1)}, f32[2,16,128]{2,1,0:T(8,128)S(1)}, u32[]{:S(2)}, u32[]{:S(2)}) %collective-permute-start.1) | collective-permute-done | bytes 16416 | tf_op jit(solution)/shard_map/ppermute | solution.py:447
  33.3 0.0 collective-permute-done.2.in2
  33.3 0.0 collective-permute-done.3.in3
  33.3 0.0 all-to-all-done
  33.3 2.8 %last.1 = f32[5,2,128,128]{3,2,1,0:T(8,128)} custom-call(f32[5,2,128,128]{3,2,1,0:T(8,128)S(1)} %get-tuple-element.20.fields_ref, f32[5,2,128,128]{3,2,1,0:T(8,128)S(1)} %get-tuple-element.21.inside_ref, f32[2,128,128]{2,1,0:T(8,128)S(1)} %get-tuple-element.22.density_ref, f32[2,2,128,128]{3,2,1,0:T(8,128)S(1)} %get-tuple-element.23.moduli_ref, ...), custom_call_target="tpu_custom_call" | custom-call | tf_op jit(solution)/shard_map/last/pallas_call | solution.py:449
Async XLA Ops:
  3.8 29.4 %all-to-all-start = ((f32[256,1,128]{2,1,0:T(1,128)}), f32[256,1,128]{2,1,0:T(1,128)S(1)}, u32[]{:S(2)}, u32[]{:S(2)}) async-start(f32[256,1,128]{2,1,0:T(1,128)} %bitcast.3), calls=%async_computation | async-start | bytes 262144 | tf_op jit(solution)/shard_map/all_to_all | solution.py:446
  18.5 9.9 %collective-permute-start = (f32[2,16,128]{2,1,0:T(8,128)S(1)}, f32[2,16,128]{2,1,0:T(8,128)S(1)}, u32[]{:S(2)}, u32[]{:S(2)}) collective-permute-start(f32[2,16,128]{2,1,0:T(8,128)S(1)} %get-tuple-element.30), channel_id=1, source_target_pairs={{0,127},{1,130},{2,129},{3,132},{4,131},{5,134},{6,133},{7,136},{8... | collective-permute-start | bytes 49160 | tf_op jit(solution)/shard_map/ppermute | solution.py:447
  25.9 7.4 %collective-permute-start.1 = (f32[2,16,128]{2,1,0:T(8,128)S(1)}, f32[2,16,128]{2,1,0:T(8,128)S(1)}, u32[]{:S(2)}, u32[]{:S(2)}) collective-permute-start(f32[2,16,128]{2,1,0:T(8,128)S(1)} %get-tuple-element.31), channel_id=1, source_target_pairs={{0,255},{1,2},{2,1},{3,4},{4,3},{5,6},{6,5},{7,8},{8,7},{9,10},{10... | collective-permute-start | bytes 49160 | tf_op jit(solution)/shard_map/ppermute | solution.py:447
  25.9 7.4 %collective-permute-start.2 = (f32[2,16,128]{2,1,0:T(8,128)S(1)}, f32[2,16,128]{2,1,0:T(8,128)S(1)}, u32[]{:S(2)}, u32[]{:S(2)}) collective-permute-start(f32[2,16,128]{2,1,0:T(8,128)S(1)} %get-tuple-element.32), channel_id=1, source_target_pairs={{0,129},{1,128},{2,131},{3,130},{4,133},{5,132},{6,135},{7,134},{8... | collective-permute-start | bytes 49160 | tf_op jit(solution)/shard_map/ppermute | solution.py:447
  25.9 7.4 %collective-permute-start.3 = (f32[2,16,128]{2,1,0:T(8,128)S(1)}, f32[2,16,128]{2,1,0:T(8,128)S(1)}, u32[]{:S(2)}, u32[]{:S(2)}) collective-permute-start(f32[2,16,128]{2,1,0:T(8,128)S(1)} %get-tuple-element.33), channel_id=1, source_target_pairs={{0,1},{1,0},{2,3},{3,2},{4,5},{5,4},{6,7},{7,6},{8,9},{9,8},{10,11... | collective-permute-start | bytes 49160 | tf_op jit(solution)/shard_map/ppermute | solution.py:447

commit v6 on v5

--- a/solution.py
+++ b/solution.py
@@ -39,7 +39,7 @@
     return (1, -1, step, -step)
 
 
-ORDER = (3, 1, 2, 0)
+ORDER = (3,0,1,2)
 
 
 def routes(total):

time: 36.2 us -> 36.2 us (level)
  starting transfers between devices: 23.7 us -> 24.5 us
  waiting for transfers between devices: 5.71 us -> 4.92 us
    ppermute x4, waiting for transfers between devices: 5.71 us -> 4.92 us  [shards(): lax.ppermute(b, PATCH_SUB, route)]
    ppermute x4, starting transfers between devices: 9.09 us -> 9.88 us  [shards(): lax.ppermute(b, PATCH_SUB, route)]
  transfers between devices with their start and end apart: 5 -> 5, of which waited for: 2 -> 1; matrix products, arithmetic and copies ran while one was open for 0% -> 0% of each run, Pallas kernels for 0% -> 0%
where the time goes in v6:
time: 36.2 us; the launch traced here: 36.1 us
  starting transfers between devices  24.5 us (68%)
  Pallas kernels  5.99 us (17%)
  waiting for transfers between devices  4.92 us (14%)
  between operations  0.68 us (2%)
    all_to_all x1, starting transfers between devices, shards(): cards = lax.all_to_all(card, PATCH_SUB, 0, 0, tiled=True)  14.6 us
    ppermute x4, starting transfers between devices, shards(): lax.ppermute(b, PATCH_SUB, route)  9.88 us
    ppermute x4, waiting for transfers between devices, shards(): lax.ppermute(b, PATCH_SUB, route)  4.92 us
    pallas_call x1, Pallas kernels, shards(): pl.pallas_call(functools.partial(front_kernel, total=total), out_shape=[b...  3.18 us
    pallas_call x1, Pallas kernels, shards(): pl.pallas_call(functools.partial(last_kernel, total=total, scale=scale),...  2.81 us
  transfers between devices with their start and end apart: 5, of which 1 were waited for; matrix products, arithmetic and copies ran while one was open for 0% of the time, Pallas kernels for 0%

profile of v6, /device:TPU:8, one launch (start us, length us, event | category | flops | bytes accessed | tf_op | source)
XLA Modules:
  0.0 36.1 jit_solution(9730785342244287783)
XLA Ops:
  0.7 3.2 %front.1 = (f32[2,16,128]{2,1,0:T(8,128)S(1)}, f32[2,16,128]{2,1,0:T(8,128)S(1)}, f32[2,16,128]{2,1,0:T(8,128)S(1)}, f32[2,16,128]{2,1,0:T(8,128)S(1)}, f32[8,16...) custom-call(f32[5,2,128,128]{3,2,1,0:T(8,128)} %fields_in.1, ...), custom_call_target="tpu_custom_call" | custom-call | tf_op jit(solution)/shard_map/front/pallas_call | solution.py:417
  3.8 14.6 %all-to-all-start = ((f32[256,1,128]{2,1,0:T(1,128)}), f32[256,1,128]{2,1,0:T(1,128)S(1)}, u32[]{:S(2)}, u32[]{:S(2)}) async-start(f32[256,1,128]{2,1,0:T(1,128)} %bitcast.3), calls=%async_computation | async-start | bytes 262144 | tf_op jit(solution)/shard_map/all_to_all | solution.py:446
  18.5 7.4 %collective-permute-start = (f32[2,16,128]{2,1,0:T(8,128)S(1)}, f32[2,16,128]{2,1,0:T(8,128)S(1)}, u32[]{:S(2)}, u32[]{:S(2)}) collective-permute-start(f32[2,16,128]{2,1,0:T(8,128)S(1)} %get-tuple-element.30), channel_id=1, source_target_pairs={{0,127},{1,130},{2,129},{3,132},{4,131},{5,134},{6,133},{7,136},{8... | collective-permute-start | bytes 49160 | tf_op jit(solution)/shard_map/ppermute | solution.py:447
  25.9 0.0 collective-permute-start.1
  25.9 2.5 %collective-permute-start.2 = (f32[2,16,128]{2,1,0:T(8,128)S(1)}, f32[2,16,128]{2,1,0:T(8,128)S(1)}, u32[]{:S(2)}, u32[]{:S(2)}) collective-permute-start(f32[2,16,128]{2,1,0:T(8,128)S(1)} %get-tuple-element.32), channel_id=1, source_target_pairs={{0,255},{1,2},{2,1},{3,4},{4,3},{5,6},{6,5},{7,8},{8,7},{9,10},{10... | collective-permute-start | bytes 49160 | tf_op jit(solution)/shard_map/ppermute | solution.py:447
  28.3 0.0 collective-permute-start.3
  28.3 0.0 collective-permute-done.in0
  28.3 0.0 collective-permute-done.1.in1
  28.4 4.9 %collective-permute-done.2.in2 = f32[2,16,128]{2,1,0:T(8,128)S(1)} collective-permute-done((f32[2,16,128]{2,1,0:T(8,128)S(1)}, f32[2,16,128]{2,1,0:T(8,128)S(1)}, u32[]{:S(2)}, u32[]{:S(2)}) %collective-permute-start.2) | collective-permute-done | bytes 16416 | tf_op jit(solution)/shard_map/ppermute | solution.py:447
  33.3 0.0 collective-permute-done.3.in3
  33.3 0.0 all-to-all-done
  33.3 2.8 %last.1 = f32[5,2,128,128]{3,2,1,0:T(8,128)} custom-call(f32[5,2,128,128]{3,2,1,0:T(8,128)S(1)} %get-tuple-element.20.fields_ref, f32[5,2,128,128]{3,2,1,0:T(8,128)S(1)} %get-tuple-element.21.inside_ref, f32[2,128,128]{2,1,0:T(8,128)S(1)} %get-tuple-element.22.density_ref, f32[2,2,128,128]{3,2,1,0:T(8,128)S(1)} %get-tuple-element.23.moduli_ref, ...), custom_call_target="tpu_custom_call" | custom-call | tf_op jit(solution)/shard_map/last/pallas_call | solution.py:449
Async XLA Ops:
  3.8 29.4 %all-to-all-start = ((f32[256,1,128]{2,1,0:T(1,128)}), f32[256,1,128]{2,1,0:T(1,128)S(1)}, u32[]{:S(2)}, u32[]{:S(2)}) async-start(f32[256,1,128]{2,1,0:T(1,128)} %bitcast.3), calls=%async_computation | async-start | bytes 262144 | tf_op jit(solution)/shard_map/all_to_all | solution.py:446
  18.5 9.9 %collective-permute-start = (f32[2,16,128]{2,1,0:T(8,128)S(1)}, f32[2,16,128]{2,1,0:T(8,128)S(1)}, u32[]{:S(2)}, u32[]{:S(2)}) collective-permute-start(f32[2,16,128]{2,1,0:T(8,128)S(1)} %get-tuple-element.30), channel_id=1, source_target_pairs={{0,127},{1,130},{2,129},{3,132},{4,131},{5,134},{6,133},{7,136},{8... | collective-permute-start | bytes 49160 | tf_op jit(solution)/shard_map/ppermute | solution.py:447
  25.9 2.5 %collective-permute-start.1 = (f32[2,16,128]{2,1,0:T(8,128)S(1)}, f32[2,16,128]{2,1,0:T(8,128)S(1)}, u32[]{:S(2)}, u32[]{:S(2)}) collective-permute-start(f32[2,16,128]{2,1,0:T(8,128)S(1)} %get-tuple-element.31), channel_id=1, source_target_pairs={{0,1},{1,0},{2,3},{3,2},{4,5},{5,4},{6,7},{7,6},{8,9},{9,8},{10,11... | collective-permute-start | bytes 49160 | tf_op jit(solution)/shard_map/ppermute | solution.py:447
  25.9 7.4 %collective-permute-start.2 = (f32[2,16,128]{2,1,0:T(8,128)S(1)}, f32[2,16,128]{2,1,0:T(8,128)S(1)}, u32[]{:S(2)}, u32[]{:S(2)}) collective-permute-start(f32[2,16,128]{2,1,0:T(8,128)S(1)} %get-tuple-element.32), channel_id=1, source_target_pairs={{0,255},{1,2},{2,1},{3,4},{4,3},{5,6},{6,5},{7,8},{8,7},{9,10},{10... | collective-permute-start | bytes 49160 | tf_op jit(solution)/shard_map/ppermute | solution.py:447
  28.3 4.9 %collective-permute-start.3 = (f32[2,16,128]{2,1,0:T(8,128)S(1)}, f32[2,16,128]{2,1,0:T(8,128)S(1)}, u32[]{:S(2)}, u32[]{:S(2)}) collective-permute-start(f32[2,16,128]{2,1,0:T(8,128)S(1)} %get-tuple-element.33), channel_id=1, source_target_pairs={{0,129},{1,128},{2,131},{3,130},{4,133},{5,132},{6,135},{7,134},{8... | collective-permute-start | bytes 49160 | tf_op jit(solution)/shard_map/ppermute | solution.py:447

commit v7 on v4

--- a/solution.py
+++ b/solution.py
@@ -13,7 +13,7 @@
 
 CFL = 0.5
 PENALTY = 0.5
-CHUNK = 16
+CHUNK = 32
 F32 = jnp.float32
 BF16 = jnp.bfloat16
 VMEM = pl.BlockSpec(memory_space=pltpu.VMEM)

time: 36.4 us -> 36.4 us (level)
  no operation moved by 1% of the time
where the time goes in v7:
time: 36.4 us; the launch traced here: 36.2 us
  starting transfers between devices  23.7 us (65%)
  Pallas kernels  6.15 us (17%)
  waiting for transfers between devices  5.71 us (16%)
  between operations  0.68 us (2%)
    all_to_all x1, starting transfers between devices, shards(): cards = lax.all_to_all(card, PATCH_SUB, 0, 0, tiled=True)  14.6 us
    ppermute x4, starting transfers between devices, shards(): lax.ppermute(b, PATCH_SUB, route)  9.09 us
    ppermute x4, waiting for transfers between devices, shards(): lax.ppermute(b, PATCH_SUB, route)  5.71 us
    pallas_call x1, Pallas kernels, shards(): pl.pallas_call(functools.partial(front_kernel, total=total), out_shape=[b...  3.18 us
    pallas_call x1, Pallas kernels, shards(): pl.pallas_call(functools.partial(last_kernel, total=total, scale=scale),...  2.97 us
  transfers between devices with their start and end apart: 5, of which 2 were waited for; matrix products, arithmetic and copies ran while one was open for 0% of the time, Pallas kernels for 0%

profile of v7, /device:TPU:8, one launch (start us, length us, event | category | flops | bytes accessed | tf_op | source)
XLA Modules:
  0.0 36.2 jit_solution(15537796160530352693)
XLA Ops:
  0.7 3.2 %front.1 = (f32[2,16,128]{2,1,0:T(8,128)S(1)}, f32[2,16,128]{2,1,0:T(8,128)S(1)}, f32[2,16,128]{2,1,0:T(8,128)S(1)}, f32[2,16,128]{2,1,0:T(8,128)S(1)}, f32[8,16...) custom-call(f32[5,2,128,128]{3,2,1,0:T(8,128)} %fields_in.1, ...), custom_call_target="tpu_custom_call" | custom-call | tf_op jit(solution)/shard_map/front/pallas_call | solution.py:417
  3.8 14.6 %all-to-all-start = ((f32[256,1,128]{2,1,0:T(1,128)}), f32[256,1,128]{2,1,0:T(1,128)S(1)}, u32[]{:S(2)}, u32[]{:S(2)}) async-start(f32[256,1,128]{2,1,0:T(1,128)} %bitcast.3), calls=%async_computation | async-start | bytes 262144 | tf_op jit(solution)/shard_map/all_to_all | solution.py:446
  18.5 7.4 %collective-permute-start = (f32[2,16,128]{2,1,0:T(8,128)S(1)}, f32[2,16,128]{2,1,0:T(8,128)S(1)}, u32[]{:S(2)}, u32[]{:S(2)}) collective-permute-start(f32[2,16,128]{2,1,0:T(8,128)S(1)} %get-tuple-element.30), channel_id=1, source_target_pairs={{0,127},{1,130},{2,129},{3,132},{4,131},{5,134},{6,133},{7,136},{8... | collective-permute-start | bytes 49160 | tf_op jit(solution)/shard_map/ppermute | solution.py:447
  25.9 0.0 collective-permute-start.1
  25.9 0.0 collective-permute-start.2
  25.9 1.7 %collective-permute-start.3 = (f32[2,16,128]{2,1,0:T(8,128)S(1)}, f32[2,16,128]{2,1,0:T(8,128)S(1)}, u32[]{:S(2)}, u32[]{:S(2)}) collective-permute-start(f32[2,16,128]{2,1,0:T(8,128)S(1)} %get-tuple-element.33), channel_id=1, source_target_pairs={{0,1},{1,0},{2,3},{3,2},{4,5},{5,4},{6,7},{7,6},{8,9},{9,8},{10,11... | collective-permute-start | bytes 49160 | tf_op jit(solution)/shard_map/ppermute | solution.py:447
  27.6 0.8 %collective-permute-done.in0 = f32[2,16,128]{2,1,0:T(8,128)S(1)} collective-permute-done((f32[2,16,128]{2,1,0:T(8,128)S(1)}, f32[2,16,128]{2,1,0:T(8,128)S(1)}, u32[]{:S(2)}, u32[]{:S(2)}) %collective-permute-start) | collective-permute-done | bytes 16416 | tf_op jit(solution)/shard_map/ppermute | solution.py:447
  28.3 4.9 %collective-permute-done.1.in1 = f32[2,16,128]{2,1,0:T(8,128)S(1)} collective-permute-done((f32[2,16,128]{2,1,0:T(8,128)S(1)}, f32[2,16,128]{2,1,0:T(8,128)S(1)}, u32[]{:S(2)}, u32[]{:S(2)}) %collective-permute-start.1) | collective-permute-done | bytes 16416 | tf_op jit(solution)/shard_map/ppermute | solution.py:447
  33.3 0.0 collective-permute-done.2.in2
  33.3 0.0 collective-permute-done.3.in3
  33.3 0.0 all-to-all-done
  33.3 3.0 %last.1 = f32[5,2,128,128]{3,2,1,0:T(8,128)} custom-call(f32[5,2,128,128]{3,2,1,0:T(8,128)S(1)} %get-tuple-element.20.fields_ref, f32[5,2,128,128]{3,2,1,0:T(8,128)S(1)} %get-tuple-element.21.inside_ref, f32[2,128,128]{2,1,0:T(8,128)S(1)} %get-tuple-element.22.density_ref, f32[2,2,128,128]{3,2,1,0:T(8,128)S(1)} %get-tuple-element.23.moduli_ref, ...), custom_call_target="tpu_custom_call" | custom-call | tf_op jit(solution)/shard_map/last/pallas_call | solution.py:449
Async XLA Ops:
  3.8 29.4 %all-to-all-start = ((f32[256,1,128]{2,1,0:T(1,128)}), f32[256,1,128]{2,1,0:T(1,128)S(1)}, u32[]{:S(2)}, u32[]{:S(2)}) async-start(f32[256,1,128]{2,1,0:T(1,128)} %bitcast.3), calls=%async_computation | async-start | bytes 262144 | tf_op jit(solution)/shard_map/all_to_all | solution.py:446
  18.5 9.9 %collective-permute-start = (f32[2,16,128]{2,1,0:T(8,128)S(1)}, f32[2,16,128]{2,1,0:T(8,128)S(1)}, u32[]{:S(2)}, u32[]{:S(2)}) collective-permute-start(f32[2,16,128]{2,1,0:T(8,128)S(1)} %get-tuple-element.30), channel_id=1, source_target_pairs={{0,127},{1,130},{2,129},{3,132},{4,131},{5,134},{6,133},{7,136},{8... | collective-permute-start | bytes 49160 | tf_op jit(solution)/shard_map/ppermute | solution.py:447
  25.9 7.4 %collective-permute-start.1 = (f32[2,16,128]{2,1,0:T(8,128)S(1)}, f32[2,16,128]{2,1,0:T(8,128)S(1)}, u32[]{:S(2)}, u32[]{:S(2)}) collective-permute-start(f32[2,16,128]{2,1,0:T(8,128)S(1)} %get-tuple-element.31), channel_id=1, source_target_pairs={{0,255},{1,2},{2,1},{3,4},{4,3},{5,6},{6,5},{7,8},{8,7},{9,10},{10... | collective-permute-start | bytes 49160 | tf_op jit(solution)/shard_map/ppermute | solution.py:447
  25.9 7.4 %collective-permute-start.2 = (f32[2,16,128]{2,1,0:T(8,128)S(1)}, f32[2,16,128]{2,1,0:T(8,128)S(1)}, u32[]{:S(2)}, u32[]{:S(2)}) collective-permute-start(f32[2,16,128]{2,1,0:T(8,128)S(1)} %get-tuple-element.32), channel_id=1, source_target_pairs={{0,129},{1,128},{2,131},{3,130},{4,133},{5,132},{6,135},{7,134},{8... | collective-permute-start | bytes 49160 | tf_op jit(solution)/shard_map/ppermute | solution.py:447
  25.9 7.4 %collective-permute-start.3 = (f32[2,16,128]{2,1,0:T(8,128)S(1)}, f32[2,16,128]{2,1,0:T(8,128)S(1)}, u32[]{:S(2)}, u32[]{:S(2)}) collective-permute-start(f32[2,16,128]{2,1,0:T(8,128)S(1)} %get-tuple-element.33), channel_id=1, source_target_pairs={{0,1},{1,0},{2,3},{3,2},{4,5},{5,4},{6,7},{7,6},{8,9},{9,8},{10,11... | collective-permute-start | bytes 49160 | tf_op jit(solution)/shard_map/ppermute | solution.py:447
